TPU v7x, 32 devices: a whole 2x2x4 slice. The times are simulated.
32 devices in a mesh: seq: 8 (over z, x), batch: 4 (over y, core).
Axes of the slice: x: 2, y: 2, z: 4, core: 2. Of those that a mesh axis runs over, the one named last changes fastest.
Arguments:
- tokens: bfloat16 [8, 1024, 768], P('batch', 'seq'), may hold values from -6 to 6
- cotangent: bfloat16 [8, 1024, 768], P('batch', 'seq'), may hold values from -6 to 6
- lengths: int32 [8], P('batch'), may hold values from 128 to 1024, as said below
- mixer_gain: bfloat16 [768], P(('seq', 'batch')), may hold values from 0.5 to 1.5
- mixer_inputs: bfloat16 [768, 2304], P(('seq', 'batch')), may hold values from -0.21875 to 0.21875
- shift_taps: bfloat16 [768, 4], P(('seq', 'batch')), may hold values from -3 to 3
- decay_rate: bfloat16 [768, 64], P(('seq', 'batch')), may hold values from 9.765625e-05 to 0.5
- state_in: bfloat16 [768, 64], P(('seq', 'batch')), may hold values from -3 to 3
- state_out: bfloat16 [768, 64], P(('seq', 'batch')), may hold values from -0.75 to 0.75
- state_skip: bfloat16 [768], P(('seq', 'batch')), may hold values from -4 to 4
- mixer_output: bfloat16 [768, 768], P(('seq', 'batch')), may hold values from -0.21875 to 0.21875
- first_gain: bfloat16 [768], P(('seq', 'batch')), may hold values from 0.5 to 1.5
- first_up: bfloat16 [768, 3072], P(('seq', 'batch')), may hold values from -0.21875 to 0.21875
- first_down: bfloat16 [3072, 768], P(('seq', 'batch')), may hold values from -0.109375 to 0.109375
- attend_gain: bfloat16 [768], P(('seq', 'batch')), may hold values from 0.5 to 1.5
- attend_inputs: bfloat16 [768, 2304], P(('seq', 'batch')), may hold values from -0.21875 to 0.21875
- attend_output: bfloat16 [768, 768], P(('seq', 'batch')), may hold values from -1.75 to 1.75
- second_gain: bfloat16 [768], P(('seq', 'batch')), may hold values from 0.5 to 1.5
- second_up: bfloat16 [768, 3072], P(('seq', 'batch')), may hold values from -0.21875 to 0.21875
- second_down: bfloat16 [3072, 768], P(('seq', 'batch')), may hold values from -0.109375 to 0.109375
Outputs:
- mixed: bfloat16 [8, 1024, 768], P('batch', 'seq')
- tokens_gradient: bfloat16 [8, 1024, 768], P('batch', 'seq')
- mixer_gain_gradient: float32 [768], P(('seq', 'batch'))
- mixer_inputs_gradient: float32 [768, 2304], P(('seq', 'batch'))
- shift_taps_gradient: float32 [768, 4], P(('seq', 'batch'))
- decay_rate_gradient: float32 [768, 64], P(('seq', 'batch'))
- state_in_gradient: float32 [768, 64], P(('seq', 'batch'))
- state_out_gradient: float32 [768, 64], P(('seq', 'batch'))
- state_skip_gradient: float32 [768], P(('seq', 'batch'))
- mixer_output_gradient: float32 [768, 768], P(('seq', 'batch'))
- first_gain_gradient: float32 [768], P(('seq', 'batch'))
- first_up_gradient: float32 [768, 3072], P(('seq', 'batch'))
- first_down_gradient: float32 [3072, 768], P(('seq', 'batch'))
- attend_gain_gradient: float32 [768], P(('seq', 'batch'))
- attend_inputs_gradient: float32 [768, 2304], P(('seq', 'batch'))
- attend_output_gradient: float32 [768, 768], P(('seq', 'batch'))
- second_gain_gradient: float32 [768], P(('seq', 'batch'))
- second_up_gradient: float32 [768, 3072], P(('seq', 'batch'))
- second_down_gradient: float32 [3072, 768], P(('seq', 'batch'))
Inputs may be any that keep to these rules, and one draw needn't show every extreme that they name: `lengths`: both ends are reached in every draw.
All inputs are finite; a program needn't handle non-finite values.
Results may differ from a plain program's by a relative error of at most 0.03.
Values may be sent and summed in bfloat16 or wider, within the bound.
A program may use at most 640 MiB of HBM per device.

v0:
```python
import functools

import jax
import jax.numpy as jnp
from jax import lax
from jax.experimental import pallas as pl
from jax.experimental.pallas import tpu as pltpu
from jax.sharding import PartitionSpec as P

HEADS = 12
HEAD_DIM = 64

eps = 1e-05
masked_score = -1e30
lanes = 128
sublanes = 8
everyone = ("seq", "batch")
f32 = jnp.float32
bf16 = jnp.bfloat16


def rows_of(ref, seq, block):
    return ref[seq, pl.ds(pl.multiple_of(block * sublanes, sublanes), sublanes), :]


def spread(rows, index, count):
    return jnp.broadcast_to(rows[index : index + 1], (count, lanes))


def encode_kernel(reverse, input_ref, decay_ref, end_ref):
    seq_count, step_count, _ = input_ref.shape
    state_count = decay_ref.shape[0]
    blocks = step_count // sublanes
    power = jnp.exp(-decay_ref[...])

    def one_block(step, states):
        block = blocks - 1 - step if reverse else step
        rows = [rows_of(input_ref, seq, block) for seq in range(seq_count)]
        order = range(sublanes - 1, -1, -1) if reverse else range(sublanes)
        states = list(states)
        for index in order:
            for seq in range(seq_count):
                states[seq] = states[seq] * power + spread(rows[seq], index, state_count)
        return tuple(states)

    start = tuple(jnp.zeros((state_count, lanes), f32) for _ in range(seq_count))
    ends = lax.fori_loop(0, blocks, one_block, start)
    for seq in range(seq_count):
        end_ref[seq] = ends[seq]


def output_kernel(input_ref, query_ref, carried_ref, decay_ref, weight_ref, skip_ref, out_ref, gated_ref):
    seq_count, step_count, _ = input_ref.shape
    state_count = decay_ref.shape[0]
    power = jnp.exp(-decay_ref[...])
    weight = weight_ref[...]
    skip = skip_ref[...]

    def one_block(block, states):
        states = list(states)
        rows = [rows_of(input_ref, seq, block) for seq in range(seq_count)]
        found = [[] for _ in range(seq_count)]
        for index in range(sublanes):
            for seq in range(seq_count):
                states[seq] = states[seq] * power + spread(rows[seq], index, state_count)
                found[seq].append(jnp.sum(states[seq] * weight, axis=0, keepdims=True))
        place = pl.ds(pl.multiple_of(block * sublanes, sublanes), sublanes)
        for seq in range(seq_count):
            result = jnp.concatenate(found[seq], axis=0) + skip * rows[seq]
            out_ref[seq, place, :] = result
            gated_ref[seq, place, :] = result * rows_of(query_ref, seq, block)
        return tuple(states)

    start = tuple(carried_ref[seq].astype(f32) for seq in range(seq_count))
    lax.fori_loop(0, step_count // sublanes, one_block, start)


def back_kernel(
    input_ref,
    grad_ref,
    carried_ref,
    later_ref,
    decay_ref,
    weight_ref,
    skip_ref,
    input_grad_ref,
    weight_grad_ref,
    power_grad_ref,
    skip_grad_ref,
    held,
):
    seq_count, step_count, _ = input_ref.shape
    state_count = decay_ref.shape[0]
    blocks = step_count // sublanes
    power = jnp.exp(-decay_ref[...])
    weight = weight_ref[...]
    skip = skip_ref[...]
    seqs = range(seq_count)

    def forward_block(block, state):
        states, total, skip_total = list(state[0]), state[1], state[2]
        rows = [rows_of(input_ref, seq, block) for seq in seqs]
        grads = [rows_of(grad_ref, seq, block) for seq in seqs]
        for index in range(sublanes):
            for seq in seqs:
                held[block * sublanes + index, seq] = states[seq]
                states[seq] = states[seq] * power + spread(rows[seq], index, state_count)
                total = total + states[seq] * spread(grads[seq], index, state_count)
        for seq in seqs:
            skip_total = skip_total + rows[seq] * grads[seq]
        return (tuple(states), total, skip_total)

    zeros = jnp.zeros((state_count, lanes), f32)
    _, total, skip_total = lax.fori_loop(
        0,
        blocks,
        forward_block,
        (
            tuple(carried_ref[seq].astype(f32) for seq in seqs),
            zeros,
            jnp.zeros((sublanes, lanes), f32),
        ),
    )
    weight_grad_ref[...] = total
    skip_grad_ref[...] = jnp.sum(skip_total, axis=0, keepdims=True)

    def back_block(step, state):
        states, total = list(state[0]), state[1]
        block = blocks - 1 - step
        grads = [rows_of(grad_ref, seq, block) for seq in seqs]
        found = [[None] * sublanes for _ in seqs]
        for index in range(sublanes - 1, -1, -1):
            for seq in seqs:
                states[seq] = states[seq] * power + spread(grads[seq], index, state_count)
                found[seq][index] = jnp.sum(states[seq] * weight, axis=0, keepdims=True)
                total = total + states[seq] * held[block * sublanes + index, seq]
        place = pl.ds(pl.multiple_of(block * sublanes, sublanes), sublanes)
        for seq in seqs:
            input_grad_ref[seq, place, :] = jnp.concatenate(found[seq], axis=0) + skip * grads[seq]
        return (tuple(states), total)

    _, total = lax.fori_loop(
        0, blocks, back_block, (tuple(later_ref[seq].astype(f32) for seq in seqs), zeros)
    )
    power_grad_ref[...] = total * weight


def per_lane_tile(kernel, args, outs, scratch=(), flops=0):
    def spec(shape):
        lead = len(shape) - 1
        return pl.BlockSpec(tuple(shape[:-1]) + (lanes,), lambda tile: (0,) * lead + (tile,))

    bytes_moved = sum(a.size * a.dtype.itemsize for a in args)
    return pl.pallas_call(
        kernel,
        grid=(args[0].shape[-1] // lanes,),
        in_specs=[spec(a.shape) for a in args],
        out_specs=[spec(o.shape) for o in outs],
        out_shape=list(outs),
        scratch_shapes=list(scratch),
        cost_estimate=pl.CostEstimate(flops=flops, bytes_accessed=bytes_moved, transcendentals=0),
        compiler_params=pltpu.CompilerParams(vmem_limit_bytes=48 * 1024 * 1024),
    )(*args)


def shaped(*dims, dtype=f32):
    return jax.ShapeDtypeStruct(dims, dtype)


def encode(value, decay, reverse):
    seq_count, _, width = value.shape
    (ends,) = per_lane_tile(
        functools.partial(encode_kernel, reverse),
        (value, decay),
        (shaped(seq_count, decay.shape[0], width),),
    )
    return ends


def passed_along(block, axis, distance):
    devices = range(lax.axis_size(axis))
    route = [(i - distance, i) for i in devices if i - distance in devices]
    return lax.ppermute(block, axis, route)


def carried_in(ends, decay, block_len, reverse):
    seq_count, state_count, width = ends.shape
    count = lax.axis_size("seq")
    part = state_count // count

    def exchanged(parts):
        return lax.all_to_all(parts.astype(bf16), "seq", split_axis=0, concat_axis=0, tiled=True)

    parts = ends.reshape(seq_count, count, part, width).transpose(1, 0, 2, 3)
    arrived = exchanged(parts.reshape(count, seq_count * part, width)).astype(f32)
    rates = lax.dynamic_slice_in_dim(decay, lax.axis_index("seq") * part, part, 0)
    power = jnp.tile(jnp.exp(-rates * block_len), (seq_count, 1))
    state, joined = jnp.zeros_like(arrived[0]), [None] * count
    for block in reversed(range(count)) if reverse else range(count):
        joined[block] = state
        state = power * state + arrived[block]
    back = exchanged(jnp.stack(joined))
    back = back.reshape(count, seq_count, part, width).transpose(1, 0, 2, 3)
    return back.reshape(seq_count, state_count, width)


MESH = pl.DeviceIdType.MESH
box = (4, 2, 2, 2)


def here():
    seq, batch = lax.axis_index("seq"), lax.axis_index("batch")
    return lax.div(seq, 2), lax.rem(seq, 2), lax.div(batch, 2), lax.rem(batch, 2)


def device(z, x, y, core):
    return (2 * z + x, 2 * y + core)


def line_peer(z, step):
    return lax.rem(z + step, box[0])


def greet():
    z, x, y, core = here()
    barrier = pltpu.get_barrier_semaphore()
    peers = [device(line_peer(z, step), x, y, core) for step in range(1, box[0])]
    peers += [device(z, 1 - x, y, core), device(z, x, 1 - y, core), device(z, x, y, 1 - core)]
    for peer in peers:
        pl.semaphore_signal(barrier, inc=1, device_id=peer, device_id_type=MESH)
    pl.semaphore_wait(barrier, len(peers))


def staggered(count, stages, gap):
    for turn in range(count + gap * (stages - 1)):
        for stage in reversed(range(stages)):
            chunk = turn - gap * stage
            if 0 <= chunk < count:
                yield stage, chunk


def gather_kernel(plan, gap, *refs):
    count = 1 + max(item[0] for item in plan)
    ins, outs = refs[:count], refs[count : 2 * count]
    send, receive, local = refs[2 * count :]
    z, x, y, core = here()
    greet()
    started = {}

    def push(chunk, slot, source, target, peer):
        copy = pltpu.make_async_remote_copy(
            src_ref=source,
            dst_ref=target,
            send_sem=send.at[chunk, slot],
            recv_sem=receive.at[chunk, slot],
            device_id=peer,
            device_id_type=MESH,
        )
        copy.start()
        started[chunk, slot] = copy

    own = []
    for chunk, (index, first, width, _) in enumerate(plan):
        columns = pl.ds(first, width)
        source = ins[index].at[:, columns]
        target = outs[index].at[z, x, y, core, :, columns]
        for step in range(1, box[0]):
            push(chunk, step - 1, source, target, device(line_peer(z, step), x, y, core))
        keep = pltpu.make_async_copy(source, target, local.at[chunk])
        keep.start()
        own.append(keep)

    for stage, chunk in staggered(len(plan), 3, gap):
        index, first, width, order = plan[chunk]
        x_first = order[1] == "x"
        columns = pl.ds(first, width)
        out = outs[index]
        if stage == 0:
            for step in range(1, box[0]):
                started[chunk, step - 1].wait_recv()
            own[chunk].wait()
            part = out.at[:, x, y, core, :, columns]
            peer = device(z, 1 - x, y, core) if x_first else device(z, x, 1 - y, core)
            push(chunk, 3, part, part, peer)
        elif stage == 1:
            started[chunk, 3].wait_recv()
            if x_first:
                part, peer = out.at[:, :, y, core, :, columns], device(z, x, 1 - y, core)
            else:
                part, peer = out.at[:, x, :, core, :, columns], device(z, 1 - x, y, core)
            push(chunk, 4, part, part, peer)
        else:
            started[chunk, 4].wait_recv()
            part = out.at[:, :, :, core, :, columns]
            push(chunk, 5, part, part, device(z, x, y, 1 - core))
    for chunk in range(len(plan)):
        started[chunk, 5].wait_recv()
        for slot in range(6):
            started[chunk, slot].wait_send()


def gather_blocks(blocks, plan, gap=2, collective=0):
    outs = [jax.ShapeDtypeStruct(box + b.shape, b.dtype) for b in blocks]
    sent = sum(b.size * b.dtype.itemsize for b in blocks)
    whole = pl.pallas_call(
        functools.partial(gather_kernel, plan, gap),
        out_shape=outs,
        in_specs=[pl.BlockSpec(memory_space=pltpu.VMEM)] * len(blocks),
        out_specs=[pl.BlockSpec(memory_space=pl.ANY)] * len(blocks),
        scratch_shapes=[
            pltpu.SemaphoreType.DMA((len(plan), 6)),
            pltpu.SemaphoreType.DMA((len(plan), 6)),
            pltpu.SemaphoreType.DMA((len(plan),)),
        ],
        cost_estimate=pl.CostEstimate(flops=0, bytes_accessed=64 * sent, transcendentals=0),
        compiler_params=pltpu.CompilerParams(collective_id=collective, has_side_effects=True),
    )(*blocks)
    return [w.reshape((32 * w.shape[4], w.shape[5])) for w in whole]


def add_into(total, other):
    return (total.astype(f32) + other.astype(f32)).astype(bf16)


def scatter_kernel(plan, gap, finish, counts, *refs):
    count, out_count = counts
    ins, results = refs[:count], refs[count : count + out_count]
    outs, buffers = refs[count + out_count : 2 * count + out_count], refs[2 * count + out_count : -3]
    send, receive, local = refs[-3:]
    z, x, y, core = here()
    greet()
    started = {}

    def push(chunk, slot, source, target, peer):
        copy = pltpu.make_async_remote_copy(
            src_ref=source,
            dst_ref=target,
            send_sem=send.at[chunk, slot],
            recv_sem=receive.at[chunk, slot],
            device_id=peer,
            device_id_type=MESH,
        )
        copy.start()
        started[chunk, slot] = copy

    loads = []
    for chunk, (index, first, width, _) in enumerate(plan):
        columns = pl.ds(first, width)
        held, from_core = buffers[5 * chunk : 5 * chunk + 2]
        grad = ins[index]
        push(chunk, 0, grad.at[:, :, :, 1 - core, :, columns], from_core, device(z, x, y, 1 - core))
        load = pltpu.make_async_copy(grad.at[:, :, :, core, :, columns], held, local.at[chunk])
        load.start()
        loads.append(load)

    for stage, chunk in staggered(len(plan), 4, gap):
        index, first, width, order = plan[chunk]
        x_first, line_last = order[0] == "y", order[-1] == "z"
        held, from_core, from_one, from_two, from_line = buffers[5 * chunk : 5 * chunk + 5]
        to_x, to_y = device(z, 1 - x, y, core), device(z, x, 1 - y, core)
        if stage == 0:
            started[chunk, 0].wait_recv()
            loads[chunk].wait()

            @pl.loop(0, box[0])
            def _(row):
                for i in range(2):
                    for j in range(2):
                        held[row, i, j] = add_into(held[row, i, j], from_core[row, i, j])

            if x_first:
                push(chunk, 1, held.at[:, :, 1 - y], from_one, to_y)
            else:
                push(chunk, 1, held.at[:, 1 - x], from_one, to_x)
        elif stage == 1:
            started[chunk, 1].wait_recv()

            @pl.loop(0, box[0])
            def _(row):
                for i in range(2):
                    if x_first:
                        held[row, i, y] = add_into(held[row, i, y], from_one[row, i])
                    else:
                        held[row, x, i] = add_into(held[row, x, i], from_one[row, i])

            if not line_last:
                for step in range(1, box[0]):
                    peer = line_peer(z, step)
                    rest = held.at[peer, :, y] if x_first else held.at[peer, x]
                    push(chunk, 2 + step, rest, from_line.at[step - 1], device(peer, x, y, core))
            elif x_first:
                push(chunk, 2, held.at[:, 1 - x, y], from_two, to_x)
            else:
                push(chunk, 2, held.at[:, x, 1 - y], from_two, to_y)
        elif stage == 2 and not line_last:
            for step in range(1, box[0]):
                started[chunk, 2 + step].wait_recv()
            for i in range(2):
                at = (z, i, y) if x_first else (z, x, i)
                total = held[at].astype(f32)
                for step in range(1, box[0]):
                    total = total + from_line[step - 1, i].astype(f32)
                held[at] = total.astype(bf16)
            if x_first:
                push(chunk, 2, held.at[z, 1 - x, y], from_two, to_x)
            else:
                push(chunk, 2, held.at[z, x, 1 - y], from_two, to_y)
        elif stage == 2:
            started[chunk, 2].wait_recv()

            @pl.loop(0, box[0])
            def _(row):
                held[row, x, y] = add_into(held[row, x, y], from_two[row])

            for step in range(1, box[0]):
                peer = line_peer(z, step)
                push(chunk, 2 + step, held.at[peer, x, y], from_line.at[step - 1], device(peer, x, y, core))
        else:
            total = held[z, x, y].astype(f32)
            if line_last:
                for step in range(1, box[0]):
                    started[chunk, 2 + step].wait_recv()
                    total = total + from_line[step - 1].astype(f32)
            else:
                started[chunk, 2].wait_recv()
                total = total + from_two[...].astype(f32)
            outs[index][:, pl.ds(first, width)] = total
            if not any(item[0] == index for item in plan[chunk + 1 :]):
                finish(index, outs[index], results)
    for chunk in range(len(plan)):
        for slot in range(6):
            started[chunk, slot].wait_send()


def scatter_blocks(grads, plan, finish, results, gap=2, collective=1):
    views = [g.reshape(box + (g.shape[0] // 32, g.shape[1])) for g in grads]
    scratch = [pltpu.VMEM(v.shape[4:], f32) for v in views]
    for index, _, width, order in plan:
        tile = (views[index].shape[4], width)
        ends_of = ((4,), (3,)) if order[-1] == "z" else ((), (3, 2))
        for lead in ((4, 2, 2), (4, 2, 2), (4, 2)) + ends_of:
            scratch.append(pltpu.VMEM(lead + tile, bf16))
    sent = sum(v.size * v.dtype.itemsize for v in views)
    return pl.pallas_call(
        functools.partial(scatter_kernel, plan, gap, finish, (len(views), len(results))),
        out_shape=list(results),
        in_specs=[pl.BlockSpec(memory_space=pl.ANY)] * len(views),
        out_specs=[pl.BlockSpec(memory_space=pltpu.VMEM)] * len(results),
        scratch_shapes=scratch
        + [
            pltpu.SemaphoreType.DMA((len(plan), 6)),
            pltpu.SemaphoreType.DMA((len(plan), 6)),
            pltpu.SemaphoreType.DMA((len(plan),)),
        ],
        cost_estimate=pl.CostEstimate(flops=0, bytes_accessed=4 * sent, transcendentals=0),
        compiler_params=pltpu.CompilerParams(
            collective_id=collective, has_side_effects=True, vmem_limit_bytes=60 * 1024 * 1024
        ),
    )(*views)


def chunked(widths, pieces, orders):
    plan = []
    for index, (width, number) in enumerate(zip(widths, pieces)):
        tiles = width // lanes
        edges = [tiles * i // number for i in range(number + 1)]
        for i in range(number):
            plan.append((index, edges[i] * lanes, (edges[i + 1] - edges[i]) * lanes, orders[len(plan) % len(orders)]))
    return plan


def carry_kernel(
    reverse, input_ref, decay_ref, carried_ref, ends, outgoing, arrived, joined, final, send, receive
):
    seq_count, step_count, width = input_ref.shape
    count = lax.axis_size("seq")
    part = decay_ref.shape[0] // count
    me, batch = lax.axis_index("seq"), lax.axis_index("batch")
    others = range(1, count)
    barrier = pltpu.get_barrier_semaphore()
    for step in others:
        peer = (lax.rem(me + step, count), batch)
        pl.semaphore_signal(barrier, inc=1, device_id=peer, device_id_type=MESH)

    for tile in range(width // lanes):
        columns = slice(tile * lanes, (tile + 1) * lanes)
        encode_kernel(reverse, input_ref.at[:, :, columns], decay_ref.at[:, columns], ends)
        for group in range(count):
            rows = slice(group * part, (group + 1) * part)
            mine = jnp.concatenate([ends[seq, rows] for seq in range(seq_count)], axis=0)
            outgoing[group, :, columns] = mine.astype(bf16)
    pl.semaphore_wait(barrier, count - 1)

    def exchange(phase, source, target):
        copies = []
        for step in others:
            peer = lax.rem(me + step, count)
            copy = pltpu.make_async_remote_copy(
                src_ref=source.at[peer],
                dst_ref=target.at[me],
                send_sem=send.at[phase, step - 1],
                recv_sem=receive.at[phase, step - 1],
                device_id=(peer, batch),
                device_id_type=MESH,
            )
            copy.start()
            copies.append(copy)
        target[me] = source[me]
        for copy in copies:
            copy.wait()

    exchange(0, outgoing, arrived)
    rates = decay_ref[pl.ds(pl.multiple_of(me * part, part), part), :]
    power = jnp.exp(-rates * step_count)
    power = jnp.concatenate([power] * seq_count, axis=0)
    state = jnp.zeros(power.shape, f32)
    for block in reversed(range(count)) if reverse else range(count):
        joined[block] = state.astype(bf16)
        state = power * state + arrived[block].astype(f32)
    exchange(1, joined, final)
    for group in range(count):
        rows = slice(group * part, (group + 1) * part)
        found = final[group].astype(f32)
        for seq in range(seq_count):
            carried_ref[seq, rows] = found[seq * part : (seq + 1) * part]


def carried_by_kernel(value, decay, reverse, collective):
    seq_count, _, width = value.shape
    state_count = decay.shape[0]
    count = lax.axis_size("seq")
    parts = pltpu.VMEM((count, seq_count * state_count // count, width), bf16)
    return pl.pallas_call(
        functools.partial(carry_kernel, reverse),
        out_shape=shaped(seq_count, state_count, width),
        in_specs=[pl.BlockSpec(memory_space=pltpu.VMEM)] * 2,
        out_specs=pl.BlockSpec(memory_space=pltpu.VMEM),
        scratch_shapes=[pltpu.VMEM((seq_count, state_count, lanes), f32)]
        + [parts] * 4
        + [pltpu.SemaphoreType.DMA((2, count - 1)), pltpu.SemaphoreType.DMA((2, count - 1))],
        cost_estimate=pl.CostEstimate(flops=0, bytes_accessed=32 * value.size, transcendentals=0),
        compiler_params=pltpu.CompilerParams(collective_id=collective, has_side_effects=True),
    )(value, decay)


hidden_block = 768
gelu_scale = 0.7978845608
gelu_cubic = 0.044715


def feed_kernel(resid_ref, gain_ref, up_ref, down_ref, out_ref, normed_ref, hidden_ref, active_ref):
    @pl.when(pl.program_id(0) == 0)
    def _():
        resid = resid_ref[...]
        normed_ref[...] = layer_norm(resid, gain_ref[...]).astype(bf16)
        out_ref[...] = resid

    hidden = jnp.dot(normed_ref[...], up_ref[...], preferred_element_type=f32)
    hidden_ref[...] = hidden
    bend = jnp.tanh(gelu_scale * (hidden + gelu_cubic * hidden * hidden * hidden))
    active = (0.5 * hidden * (1.0 + bend)).astype(bf16)
    active_ref[...] = active
    out_ref[...] += jnp.dot(active, down_ref[...], preferred_element_type=f32)


def feed_forward_blocks(resid, gain, up_packed, up_at, down):
    rows, width = resid.shape
    inner = down.shape[0]
    first = up_at // hidden_block
    whole = pl.BlockSpec((rows, width), lambda j: (0, 0))
    part = pl.BlockSpec((rows, hidden_block), lambda j: (0, j))
    out, normed, hidden, active = pl.pallas_call(
        feed_kernel,
        grid=(inner // hidden_block,),
        in_specs=[
            whole,
            pl.BlockSpec((1, width), lambda j: (0, 0)),
            pl.BlockSpec((width, hidden_block), lambda j: (0, first + j)),
            pl.BlockSpec((hidden_block, width), lambda j: (j, 0)),
        ],
        out_specs=[whole, whole, part, part],
        out_shape=[
            shaped(rows, width),
            shaped(rows, width, dtype=bf16),
            shaped(rows, inner),
            shaped(rows, inner, dtype=bf16),
        ],
        cost_estimate=pl.CostEstimate(
            flops=4 * rows * width * inner, bytes_accessed=10 * width * inner, transcendentals=rows * inner
        ),
        compiler_params=pltpu.CompilerParams(vmem_limit_bytes=40 * 1024 * 1024),
    )(resid, gain[None], up_packed, down)
    return out, (resid, gain, normed, hidden, active)


def feed_back_kernel(
    packed,
    upstream_ref,
    resid_ref,
    gain_ref,
    normed_ref,
    hidden_ref,
    active_ref,
    up_ref,
    down_ref,
    out_ref,
    gain_grad_ref,
    *rest,
):
    step = pl.program_id(0)
    last = pl.num_programs(0) - 1
    across = (((1,), (1,)), ((), ()))
    along = (((0,), (0,)), ((), ()))
    upstream_low = upstream_ref[...].astype(bf16)
    into_active = lax.dot_general(upstream_low, down_ref[...], across, preferred_element_type=f32)
    hidden = hidden_ref[...]
    square = hidden * hidden
    bend = jnp.tanh(gelu_scale * hidden * (1.0 + gelu_cubic * square))
    slope = 0.5 * (1.0 + bend) + 0.5 * hidden * (1.0 - bend * bend) * (
        gelu_scale * (1.0 + 3.0 * gelu_cubic * square)
    )
    into_hidden = (into_active * slope).astype(bf16)
    part = lax.dot_general(into_hidden, up_ref[...], across, preferred_element_type=f32)

    @pl.when(step == 0)
    def _():
        out_ref[...] = part

    @pl.when(step > 0)
    def _():
        out_ref[...] += part

    up_grad = lax.dot_general(normed_ref[...], into_hidden, along, preferred_element_type=f32)
    down_grad = lax.dot_general(active_ref[...], upstream_low, along, preferred_element_type=f32)
    if packed:
        grads_ref, up_held, down_held, sems = rest
        share, fold = packed
        width = up_grad.shape[0]
        inner = hidden_block * grads_ref.shape[1] // (2 * hidden_block)
        tall = hidden_block // fold
        slot = lax.rem(step, 2)

        def copies(at, slot):
            columns = pl.ds(pl.multiple_of(at * hidden_block, hidden_block), hidden_block)
            rows = pl.ds(pl.multiple_of(at * tall, tall), tall)
            return (
                pltpu.make_async_copy(up_held.at[slot], grads_ref.at[:, columns], sems.at[0, slot]),
                pltpu.make_async_copy(down_held.at[slot], grads_ref.at[rows, inner:], sems.at[1, slot]),
            )

        @pl.when(step >= 2)
        def _():
            for copy in copies(step - 2, slot):
                copy.wait()

        up_held[slot] = up_grad.astype(bf16)
        for place in range(fold):
            starts = range(place * share, hidden_block, fold * share)
            piece = jnp.concatenate([down_grad[a : a + share] for a in starts], axis=0)
            down_held[slot, :, place * width : (place + 1) * width] = piece.astype(bf16)
        for copy in copies(step, slot):
            copy.start()

        @pl.when(step == last)
        def _():
            for copy in copies(step - 1, 1 - slot) + copies(step, slot):
                copy.wait()
    else:
        up_grad_ref, down_grad_ref = rest
        up_grad_ref[...] = up_grad.astype(bf16)
        down_grad_ref[...] = down_grad.astype(bf16)

    @pl.when(step == last)
    def _():
        into_normed = out_ref[...]
        resid = resid_ref[...]
        centred = resid - jnp.mean(resid, axis=-1, keepdims=True)
        inverse = lax.rsqrt(jnp.mean(centred * centred, axis=-1, keepdims=True) + eps)
        unit = centred * inverse
        gain_grad_ref[...] = jnp.sum(into_normed * unit, axis=0, keepdims=True)
        scaled = into_normed * gain_ref[...]
        along_unit = jnp.mean(scaled * unit, axis=-1, keepdims=True)
        into_resid = inverse * (scaled - jnp.mean(scaled, axis=-1, keepdims=True) - unit * along_unit)
        out_ref[...] = upstream_ref[...] + into_resid


def feed_back_blocks(stored, up_packed, up_at, down, upstream, packed=()):
    resid, gain, normed, hidden, active = stored
    rows, width = resid.shape
    inner = down.shape[0]
    first = up_at // hidden_block
    whole = pl.BlockSpec((rows, width), lambda j: (0, 0))
    part = pl.BlockSpec((rows, hidden_block), lambda j: (0, j))
    line = pl.BlockSpec((1, width), lambda j: (0, 0))
    up_spec = pl.BlockSpec((width, hidden_block), lambda j: (0, j))
    down_spec = pl.BlockSpec((hidden_block, width), lambda j: (j, 0))
    scratch = []
    if packed:
        grad_specs = [pl.BlockSpec(memory_space=pl.ANY)]
        grad_shapes = [shaped(width, 2 * inner, dtype=bf16)]
        scratch = [
            pltpu.VMEM((2, width, hidden_block), bf16),
            pltpu.VMEM((2, hidden_block // packed[1], inner), bf16),
            pltpu.SemaphoreType.DMA((2, 2)),
        ]
    else:
        grad_specs = [up_spec, down_spec]
        grad_shapes = [shaped(width, inner, dtype=bf16), shaped(inner, width, dtype=bf16)]
    out, gain_grad, *grads = pl.pallas_call(
        functools.partial(feed_back_kernel, packed),
        grid=(inner // hidden_block,),
        in_specs=[
            whole,
            whole,
            line,
            whole,
            part,
            part,
            pl.BlockSpec((width, hidden_block), lambda j: (0, first + j)),
            down_spec,
        ],
        out_specs=[whole, line] + grad_specs,
        out_shape=[shaped(rows, width), shaped(1, width)] + grad_shapes,
        scratch_shapes=scratch,
        cost_estimate=pl.CostEstimate(
            flops=8 * rows * width * inner, bytes_accessed=16 * width * inner, transcendentals=rows * inner
        ),
        compiler_params=pltpu.CompilerParams(vmem_limit_bytes=48 * 1024 * 1024),
    )(upstream, resid, gain[None], normed, hidden, active, up_packed, down)
    return (out, gain_grad[0], *grads)


def split_heads(ref, scratch, heads, parts, first=0):
    for part in range(parts):
        for head in range(heads):
            start = (part * heads + head) * HEAD_DIM + first
            scratch[part * heads + head] = ref[:, start : start + HEAD_DIM]


def score_block(query, keys, first, scale):
    scores = (
        lax.dot_general(query, keys, (((1,), (1,)), ((), ())), preferred_element_type=f32) * scale
    )
    rows = lax.broadcasted_iota(jnp.int32, scores.shape, 0) + first
    columns = lax.broadcasted_iota(jnp.int32, scores.shape, 1)
    return jnp.where(columns <= rows, scores, masked_score)


def attend_kernel(heads, block, scale, qkv_ref, low_ref, full_ref, stat_ref, parts, outs):
    length = qkv_ref.shape[0]
    split_heads(qkv_ref, parts, heads, 3)

    @pl.loop(0, heads)
    def _(head):
        for first in range(0, length, block):
            extent = first + block
            query = parts[head, first:extent, :]
            scores = score_block(query, parts[heads + head, :extent, :], first, scale)
            top = jnp.max(scores, axis=1, keepdims=True)
            soft = jnp.exp(scores - top)
            whole = jnp.sum(soft, axis=1, keepdims=True)
            soft = soft * (1.0 / whole)
            outs[head, first:extent, :] = jnp.dot(
                soft.astype(bf16), parts[2 * heads + head, :extent, :], preferred_element_type=f32
            )
            stat_ref[head, first:extent, :] = jnp.broadcast_to(top + jnp.log(whole), (block, lanes))

    if low_ref.shape[1] > heads * HEAD_DIM:
        low_ref[:, heads * HEAD_DIM :] = jnp.zeros((length, low_ref.shape[1] - heads * HEAD_DIM), bf16)
    for head in range(heads):
        place = slice(head * HEAD_DIM, (head + 1) * HEAD_DIM)
        full_ref[:, place] = outs[head]
        low_ref[:, place] = outs[head].astype(bf16)


def attend_back_kernel(
    heads, block, scale, qkv_ref, dout_ref, full_ref, stat_ref, grad_ref, parts, douts, fulls, grads
):
    length = qkv_ref.shape[0]
    split_heads(qkv_ref, parts, heads, 3)
    split_heads(dout_ref, douts, heads, 1)
    split_heads(full_ref, fulls, heads, 1)
    grads[...] = jnp.zeros_like(grads)

    @pl.loop(0, heads)
    def _(head):
        for first in range(0, length, block):
            extent = first + block
            query = parts[head, first:extent, :]
            keys = parts[heads + head, :extent, :]
            value = parts[2 * heads + head, :extent, :]
            dout = douts[head, first:extent, :]
            delta = jnp.sum(dout.astype(f32) * fulls[head, first:extent, :], axis=1, keepdims=True)
            scores = score_block(query, keys, first, scale)
            soft = jnp.exp(scores - stat_ref[head, first:extent, :1])
            across = (((1,), (1,)), ((), ()))
            along = (((0,), (0,)), ((), ()))
            dprob = lax.dot_general(dout, value, across, preferred_element_type=f32)
            dscore = (soft * (dprob - delta) * scale).astype(bf16)
            grads[head, first:extent, :] = jnp.dot(dscore, keys, preferred_element_type=f32)
            grads[heads + head, :extent, :] += lax.dot_general(
                dscore, query, along, preferred_element_type=f32
            )
            grads[2 * heads + head, :extent, :] += lax.dot_general(
                soft.astype(bf16), dout, along, preferred_element_type=f32
            )

    grad_ref[...] = jnp.zeros_like(grad_ref)
    for part in range(3 * heads):
        grad_ref[:, part * HEAD_DIM : (part + 1) * HEAD_DIM] = grads[part].astype(bf16)


def attend_params():
    return pltpu.CompilerParams(vmem_limit_bytes=56 * 1024 * 1024)


def attend_whole(qkv, heads, block):
    length = qkv.shape[0]
    width = heads * HEAD_DIM
    return pl.pallas_call(
        functools.partial(attend_kernel, heads, block, HEAD_DIM ** (-0.5)),
        out_shape=[
            shaped(length, -(-width // lanes) * lanes, dtype=bf16),
            shaped(length, width),
            shaped(heads, length, lanes),
        ],
        scratch_shapes=[
            pltpu.VMEM((3 * heads, length, HEAD_DIM), bf16),
            pltpu.VMEM((heads, length, HEAD_DIM), f32),
        ],
        compiler_params=attend_params(),
    )(qkv)


def attend_whole_back(qkv, dout, full, stat, heads, block):
    length = qkv.shape[0]
    return pl.pallas_call(
        functools.partial(attend_back_kernel, heads, block, HEAD_DIM ** (-0.5)),
        out_shape=shaped(*qkv.shape, dtype=bf16),
        scratch_shapes=[
            pltpu.VMEM((3 * heads, length, HEAD_DIM), bf16),
            pltpu.VMEM((heads, length, HEAD_DIM), bf16),
            pltpu.VMEM((heads, length, HEAD_DIM), f32),
            pltpu.VMEM((3 * heads, length, HEAD_DIM), f32),
        ],
        compiler_params=attend_params(),
    )(qkv, dout, full, stat)


def split_blocks(array, block_len):
    shaped_blocks = array.reshape(
        (array.shape[0], array.shape[1] // block_len, block_len) + array.shape[2:]
    )
    return jnp.moveaxis(shaped_blocks, 1, 0)


def general_attention(proj_low, seq_count, block_len, places, any_live, longest):
    model_width = HEADS * HEAD_DIM
    scale = HEAD_DIM ** (-0.5)
    offsets = jnp.arange(block_len, dtype=jnp.int32)
    head_shape = (seq_count, block_len, HEADS, HEAD_DIM)
    query_low = proj_low[:, :model_width].reshape(head_shape)
    keys_low = proj_low[:, model_width : 2 * model_width].reshape(head_shape)
    value_low = proj_low[:, 2 * model_width :].reshape(head_shape)

    def block_scores(queries, keys_block, query_places, key_places):
        scores = (
            jnp.einsum("sqhe,skhe->sqhk", queries, keys_block, preferred_element_type=jnp.float32)
            * scale
        )
        causal_mask = key_places[None, :] <= query_places[:, None]
        return jnp.where(causal_mask[None, :, None, :], scores, masked_score)

    def key_needed(key_first):
        return (key_first <= places[-1]) & ((key_first == places[0]) | any_live)

    stat_shape = (seq_count, block_len, HEADS)
    start_state = (
        jnp.full(stat_shape, masked_score, jnp.float32),
        jnp.zeros(stat_shape, jnp.float32),
        jnp.zeros(head_shape, jnp.float32),
    )
    shard_piece = (
        lax.all_gather(keys_low, "seq", axis=1, tiled=True),
        lax.all_gather(value_low, "seq", axis=1, tiled=True),
    )
    keys_blocks = split_blocks(shard_piece[0], block_len)
    value_blocks = split_blocks(shard_piece[1], block_len)
    firsts = jnp.arange(keys_blocks.shape[0], dtype=jnp.int32) * block_len

    def attend_one_step(state_now, operand):
        keys_block, value_block, key_first = operand

        def attend_work(state_in_block):
            running_max, running_sum, running_out = state_in_block
            scores = block_scores(query_low, keys_block, places, key_first + offsets)
            new_max = jnp.maximum(running_max, jnp.max(scores, axis=-1))
            fade = jnp.exp(running_max - new_max)
            shifted = jnp.exp(scores - new_max[..., None])
            new_sum = running_sum * fade + jnp.sum(shifted, axis=-1)
            new_out = running_out * fade[..., None] + jnp.einsum(
                "sqhk,skhe->sqhe",
                shifted.astype(jnp.bfloat16),
                value_block,
                preferred_element_type=jnp.float32,
            )
            return (new_max, new_sum, new_out)

        return (
            lax.cond(
                key_needed(key_first), attend_work, lambda state_in_block: state_in_block, state_now
            ),
            None,
        )

    result, _ = lax.scan(attend_one_step, start_state, (keys_blocks, value_blocks, firsts))
    running_max, running_sum, running_out = result
    attended = running_out / running_sum[..., None]
    logsum = running_max + jnp.log(running_sum)
    def backward(dout_low):
        delta = jnp.sum(dout_low.astype(jnp.float32) * attended, axis=-1)
        shard_piece = (
            lax.all_gather(keys_low, "seq", axis=1, tiled=True),
            lax.all_gather(value_low, "seq", axis=1, tiled=True),
        )
        keys_blocks = split_blocks(shard_piece[0], block_len)
        value_blocks = split_blocks(shard_piece[1], block_len)
        firsts = jnp.arange(keys_blocks.shape[0], dtype=jnp.int32) * block_len

        def query_one_step(query_grad, operand):
            keys_block, value_block, key_first = operand

            def query_work(grad_now):
                scores = block_scores(query_low, keys_block, places, key_first + offsets)
                soft = jnp.exp(scores - logsum[..., None])
                dprob = jnp.einsum(
                    "sqhe,skhe->sqhk", dout_low, value_block, preferred_element_type=jnp.float32
                )
                dscore = (soft * (dprob - delta[..., None])).astype(jnp.bfloat16)
                return (
                    grad_now
                    + jnp.einsum(
                        "sqhk,skhe->sqhe", dscore, keys_block, preferred_element_type=jnp.float32
                    )
                    * scale
                )

            return (
                lax.cond(key_needed(key_first), query_work, lambda grad_now: grad_now, query_grad),
                None,
            )

        result, _ = lax.scan(
            query_one_step, jnp.zeros(head_shape, jnp.float32), (keys_blocks, value_blocks, firsts)
        )
        query_grad = result
        sent = (query_low.astype(jnp.float32), dout_low.astype(jnp.float32), logsum, delta)
        shard_piece = (
            lax.all_gather(sent[0].astype(jnp.bfloat16), "seq", axis=1, tiled=True).astype(jnp.float32),
            lax.all_gather(sent[1].astype(jnp.bfloat16), "seq", axis=1, tiled=True).astype(jnp.float32),
            lax.all_gather(sent[2].astype(jnp.bfloat16), "seq", axis=1, tiled=True).astype(jnp.float32),
            lax.all_gather(sent[3].astype(jnp.bfloat16), "seq", axis=1, tiled=True).astype(jnp.float32),
        )
        query_blocks = split_blocks(shard_piece[0], block_len)
        dout_blocks = split_blocks(shard_piece[1], block_len)
        logsum_blocks = split_blocks(shard_piece[2], block_len)
        delta_blocks = split_blocks(shard_piece[3], block_len)
        firsts = jnp.arange(query_blocks.shape[0], dtype=jnp.int32) * block_len

        def key_one_step(grads_now, operand):
            query_block, dout_block, logsum_block, delta_block, query_first = operand

            def key_work(grads_in):
                keys_grad, value_grad = grads_in
                query_cast = query_block.astype(jnp.bfloat16)
                dout_cast = dout_block.astype(jnp.bfloat16)
                scores = block_scores(query_cast, keys_low, query_first + offsets, places)
                soft = jnp.exp(scores - logsum_block[..., None])
                value_grad = value_grad + jnp.einsum(
                    "sqhk,sqhe->skhe",
                    soft.astype(jnp.bfloat16),
                    dout_cast,
                    preferred_element_type=jnp.float32,
                )
                dprob = jnp.einsum(
                    "sqhe,skhe->sqhk", dout_cast, value_low, preferred_element_type=jnp.float32
                )
                dscore = (soft * (dprob - delta_block[..., None])).astype(jnp.bfloat16)
                keys_grad = (
                    keys_grad
                    + jnp.einsum(
                        "sqhk,sqhe->skhe", dscore, query_cast, preferred_element_type=jnp.float32
                    )
                    * scale
                )
                return (keys_grad, value_grad)

            needed = (query_first + block_len - 1 >= places[0]) & (
                (query_first == places[0]) | (query_first < longest)
            )
            return (lax.cond(needed, key_work, lambda grads_in: grads_in, grads_now), None)

        result, _ = lax.scan(
            key_one_step,
            (jnp.zeros(head_shape, jnp.float32), jnp.zeros(head_shape, jnp.float32)),
            (query_blocks, dout_blocks, logsum_blocks, delta_blocks, firsts),
        )
        keys_grad, value_grad = result
        return (query_grad, keys_grad, value_grad)

    return attended, backward


def layer_norm(value, gain):
    centred = value - jnp.mean(value, axis=-1, keepdims=True)
    spread_of = jnp.mean(centred * centred, axis=-1, keepdims=True)
    return centred * lax.rsqrt(spread_of + eps) * gain


def gelu_tanh(value):
    return jax.nn.gelu(value, approximate=True)


def dense(left, weight):
    return jnp.dot(left, weight, preferred_element_type=f32)


def dense_back(left, weight, upstream):
    into_left = lax.dot_general(
        upstream, weight, (((1,), (1,)), ((), ())), preferred_element_type=f32
    )
    into_weight = lax.dot_general(
        left, upstream, (((0,), (0,)), ((), ())), preferred_element_type=f32
    ).astype(bf16)
    return (into_left, into_weight)


def shift_mix(extended, taps, value_part):
    step_count = value_part.shape[1]
    reach = taps.shape[1]
    shifted = extended[:, reach - 1 : reach - 1 + step_count] * taps[:, 0]
    for tap_index in range(1, reach):
        shifted = (
            shifted
            + extended[:, reach - 1 - tap_index : reach - 1 - tap_index + step_count]
            * taps[:, tap_index]
        )
    return shifted * value_part


def feed_forward(resid, gain, up_weight, down_weight):
    normed, norm_back = jax.vjp(layer_norm, resid, gain)
    normed_low = normed.astype(bf16)
    hidden = dense(normed_low, up_weight)
    active, active_back = jax.vjp(gelu_tanh, hidden)
    active_low = active.astype(bf16)
    return (
        resid + dense(active_low, down_weight),
        (norm_back, normed_low, active_back, active_low),
    )


def feed_back(stored, up_weight, down_weight, upstream):
    norm_back, normed_low, active_back, active_low = stored
    into_active, down_grad = dense_back(active_low, down_weight, upstream.astype(bf16))
    (into_hidden,) = active_back(into_active)
    into_normed, up_grad = dense_back(normed_low, up_weight, into_hidden.astype(bf16))
    into_resid, gain_grad = norm_back(into_normed)
    return (upstream + into_resid, gain_grad, up_grad, down_grad)


def fold_rows(weight, share):
    rows, width = weight.shape
    fold = rows // share
    return weight.reshape(fold, share, width).transpose(1, 0, 2).reshape(share, fold * width)


def unfold_rows(folded, fold, share):
    rows, width = folded.shape
    width //= fold
    parts = folded.reshape(rows // share, share, fold, width).transpose(0, 2, 1, 3)
    return parts.reshape(rows * fold, width)


def fold_all(weight, share, rows):
    tall, width = weight.shape
    fold = tall // rows
    parts = weight.reshape(rows // share, fold, share, width).transpose(0, 2, 1, 3)
    return parts.reshape(rows, fold * width)


def group_columns(weight, groups, padded):
    rows, columns = weight.shape
    part = columns // 3 // groups
    grouped = weight.reshape(rows, 3, groups, part).transpose(0, 2, 1, 3).reshape(rows, groups, 3 * part)
    return jnp.pad(grouped, ((0, 0), (0, 0), (0, padded - 3 * part))).reshape(rows, groups * padded)


def pad_groups(weight, groups, padded):
    rows, columns = weight.shape
    part = rows // groups
    grouped = weight.reshape(groups, part, columns)
    return jnp.pad(grouped, ((0, 0), (0, padded - part), (0, 0))).reshape(groups * padded, columns)


def ungroup_columns(grouped, groups, padded, columns):
    rows = grouped.shape[0]
    part = columns // 3 // groups
    parts = grouped.reshape(rows, groups, padded)[:, :, : 3 * part].reshape(rows, groups, 3, part)
    return parts.transpose(0, 2, 1, 3).reshape(rows, columns)


def cut(array, widths):
    pieces, start = [], 0
    for width in widths:
        pieces.append(array[:, start : start + width])
        start += width
    return pieces


def cut_last(array, count):
    width = array.shape[-1] // count
    return [array[..., i * width : (i + 1) * width] for i in range(count)]


def gathered(parts):
    whole = lax.all_gather(jnp.concatenate(parts, axis=1), everyone, axis=0, tiled=True)
    return cut(whole, [p.shape[1] for p in parts])


def scattered(parts):
    mine = lax.psum_scatter(
        jnp.concatenate(parts, axis=1), everyone, scatter_dimension=0, tiled=True
    )
    return cut(mine, [p.shape[1] for p in parts])


def body(
    tokens,
    cotangent,
    lengths,
    mixer_gain,
    mixer_inputs,
    shift_taps,
    decay_rate,
    state_in,
    state_out,
    state_skip,
    mixer_output,
    first_gain,
    first_up,
    first_down,
    attend_gain,
    attend_inputs,
    attend_output,
    second_gain,
    second_up,
    second_down,
):
    seq_count, block_len, model_width = tokens.shape
    row_count = seq_count * block_len
    seq_devices = lax.axis_size("seq")
    share = mixer_inputs.shape[0]
    states, reach = decay_rate.shape[1], shift_taps.shape[1]
    fold = first_down.shape[0] // share
    deals = seq_count * HEADS
    dealt = deals % seq_devices == 0 and HEADS % (deals // seq_devices) == 0
    heads = deals // seq_devices if dealt else HEADS
    groups = HEADS // heads
    group_width = heads * HEAD_DIM
    padded = -(-3 * group_width // lanes) * lanes if dealt else 3 * group_width
    out_width = -(-group_width // lanes) * lanes if dealt else group_width

    columns = [decay_rate, state_in, state_out, shift_taps]
    columns += [g[:, None] for g in (mixer_gain, first_gain, attend_gain, second_gain, state_skip)]
    small = jnp.concatenate(columns, axis=1)
    small_count = small.shape[1]
    small_width = -(-small_count // lanes) * lanes
    small = jnp.pad(small, ((0, 0), (0, small_width - small_count)))
    attend_cols = attend_inputs.shape[1]
    grouped = group_columns(attend_inputs, groups, padded)
    by_kernel = seq_devices == 8 and lax.axis_size("batch") == 4
    packed = [mixer_output, attend_output, first_up, second_up, grouped]
    up1_at = 2 * model_width
    up2_at = up1_at + first_up.shape[1]
    if by_kernel:
        joint = jnp.concatenate([mixer_inputs, small], axis=1)
        w_packed = lax.all_gather(jnp.concatenate(packed, axis=1), everyone, axis=0, tiled=True)
        w_mixer_out, w_attend_out, _, _, w_attend_in = cut(w_packed, [p.shape[1] for p in packed])
        widths = (joint.shape[1], model_width)
        w_joint, w_down1 = gather_blocks((joint, first_down), chunked(widths, (4, 6), ("zxy", "zyx")), gap=3)
        w_mixer_in, w_small = cut(w_joint, [mixer_inputs.shape[1], small_width])
        second_down, w_small = lax.optimization_barrier((second_down, w_small))
        w_down2 = lax.all_gather(second_down, everyone, axis=0, tiled=True)
    else:
        w_mixer_in, w_small = gathered([mixer_inputs, small])
        packed += [fold_rows(first_down, share), fold_rows(second_down, share)]
        w_mixer_out, w_attend_out, w_up1, w_up2, w_attend_in, w_down1, w_down2 = gathered(packed)
        w_down1 = unfold_rows(w_down1, fold, share)
        w_down2 = unfold_rows(w_down2, fold, share)

    rows = w_small.T.astype(f32)
    decay, table_in, table_out = rows[:states], rows[states : 2 * states], rows[2 * states : 3 * states]
    taps_rows = rows[3 * states : 3 * states + reach]
    gain_mixer, gain_first, gain_attend, gain_second, skip = (
        rows[3 * states + reach + i] for i in range(5)
    )
    taps = taps_rows.T
    weight = table_in * table_out

    rank_seq = lax.axis_index("seq")
    offsets = jnp.arange(block_len, dtype=jnp.int32)
    places = rank_seq * block_len + offsets
    valid = (places[None, :] < lengths[:, None]).astype(f32)
    longest = jnp.max(lengths)
    any_live = places[0] < longest

    start_resid = tokens.reshape(row_count, model_width).astype(f32)
    normed_mixer, back_mixer = jax.vjp(layer_norm, start_resid, gain_mixer)
    normed_low_mixer = normed_mixer.astype(bf16)
    projected = dense(normed_low_mixer, w_mixer_in).reshape(seq_count, block_len, 3 * model_width)
    query_mixer = projected[:, :, :model_width]
    keys_mixer = projected[:, :, model_width : 2 * model_width]
    value_mixer = projected[:, :, 2 * model_width :]
    rim_rows = passed_along(keys_mixer[:, block_len - reach + 1 :], "seq", 1)
    extended = jnp.concatenate([rim_rows, keys_mixer], axis=1)
    inner, shift_back = jax.vjp(shift_mix, extended, taps, value_mixer)
    if by_kernel:
        carried = carried_by_kernel(inner, decay, False, 2)
    else:
        carried = carried_in(encode(inner, decay, False), decay, block_len, False)
    wide = shaped(seq_count, block_len, model_width)
    state_y, gated = per_lane_tile(
        output_kernel,
        (inner, query_mixer, carried, decay, weight, skip[None]),
        (wide, wide),
    )
    gated_low = gated.astype(bf16).reshape(row_count, model_width)
    resid_mixer = start_resid + dense(gated_low, w_mixer_out)
    if by_kernel:
        resid_first, stored_first = feed_forward_blocks(
            resid_mixer, gain_first, w_packed, up1_at, w_down1
        )
    else:
        resid_first, stored_first = feed_forward(resid_mixer, gain_first, w_up1, w_down1)

    normed_attend, back_attend = jax.vjp(layer_norm, resid_first, gain_attend)
    normed_low_attend = normed_attend.astype(bf16)
    proj_low = dense(normed_low_attend, w_attend_in).astype(bf16)
    if dealt:
        length = seq_devices * block_len
        block = min(256, length)

        def deal(array, width):
            array = array.reshape(seq_count, block_len, groups * width)
            parts = jnp.stack(cut_last(array, groups), axis=1)
            parts = parts.reshape(seq_count * groups, block_len, width)
            dealt_parts = lax.all_to_all(parts, "seq", split_axis=0, concat_axis=0, tiled=True)
            return dealt_parts.reshape(length, width)

        def collect(array, width):
            parts = array.reshape(seq_devices, block_len, width)
            back = lax.all_to_all(parts, "seq", split_axis=0, concat_axis=0, tiled=True)
            back = back.reshape(seq_count, groups, block_len, width)
            back = jnp.concatenate([back[:, group] for group in range(groups)], axis=-1)
            return back.reshape(row_count, groups * width)

        qkv = deal(proj_low, padded)
        attended_part, attended_full, stat = attend_whole(qkv, heads, block)
        attended_low = collect(attended_part, out_width)
        w_attend_out = pad_groups(w_attend_out, groups, out_width)
    else:
        attended, attended_back = general_attention(
            proj_low, seq_count, block_len, places, any_live, longest
        )
        attended_low = attended.reshape(row_count, model_width).astype(bf16)
    resid_attend = resid_first + dense(attended_low, w_attend_out)
    if by_kernel:
        final, stored_second = feed_forward_blocks(
            resid_attend, gain_second, w_packed, up2_at, w_down2
        )
    else:
        final, stored_second = feed_forward(resid_attend, gain_second, w_up2, w_down2)
    mixed = (final.reshape(seq_count, block_len, model_width) * valid[..., None]).astype(bf16)

    upstream = (cotangent.astype(f32) * valid[..., None]).reshape(row_count, model_width)
    if by_kernel:
        upstream, second_gain_grad, early = feed_back_blocks(
            stored_second, w_packed, up2_at, w_down2, upstream, packed=(share, fold)
        )
    else:
        upstream, second_gain_grad, second_up_grad, second_down_grad = feed_back(
            stored_second, w_up2, w_down2, upstream
        )
        early = [second_up_grad, fold_all(second_down_grad, share, model_width)]
        early = jnp.concatenate(early, axis=1)
    into_attended, attend_output_grad = dense_back(
        attended_low, w_attend_out, upstream.astype(bf16)
    )
    if dealt:
        attend_output_grad = attend_output_grad.reshape(groups, out_width, model_width)
        attend_output_grad = attend_output_grad[:, :group_width].reshape(model_width, model_width)
    dout_low = into_attended.astype(bf16)
    if dealt:
        dout = deal(dout_low, out_width)
        qkv_grad = attend_whole_back(qkv, dout, attended_full, stat, heads, block)
        qkv_grad, early = lax.optimization_barrier((qkv_grad, early))
        proj_grad = collect(qkv_grad, padded)
    else:
        parts = attended_back(dout_low.reshape(seq_count, block_len, HEADS, HEAD_DIM))
        proj_grad = jnp.concatenate(
            [p.reshape(row_count, model_width) for p in parts], axis=1
        ).astype(bf16)
    early = lax.psum_scatter(early, everyone, scatter_dimension=0, tiled=True)
    second_up_out, second_down_out = cut(early, [second_up.shape[1], fold * model_width])
    into_normed, attend_inputs_grad = dense_back(normed_low_attend, w_attend_in, proj_grad)
    into_resid, attend_gain_grad = back_attend(into_normed)
    upstream = upstream + into_resid
    if by_kernel:
        upstream, first_gain_grad, first_up_grad, first_down_grad = feed_back_blocks(
            stored_first, w_packed, up1_at, w_down1, upstream
        )
    else:
        upstream, first_gain_grad, first_up_grad, first_down_grad = feed_back(
            stored_first, w_up1, w_down1, upstream
        )
    into_gated, mixer_output_grad = dense_back(gated_low, w_mixer_out, upstream.astype(bf16))
    into_gated = into_gated.reshape(seq_count, block_len, model_width)
    query_mixer_grad = into_gated * state_y
    state_grad = into_gated * query_mixer
    if by_kernel:
        later = carried_by_kernel(state_grad, decay, True, 3)
    else:
        later = carried_in(encode(state_grad, decay, True), decay, block_len, True)
    table = shaped(states, model_width)
    inner_grad, weight_grad, power_grad, skip_grad = per_lane_tile(
        back_kernel,
        (inner, state_grad, carried, later, decay, weight, skip[None]),
        (wide, table, table, shaped(1, model_width)),
        scratch=[pltpu.VMEM((block_len, seq_count, states, lanes), f32)],
    )
    extended_grad, taps_grad, value_mixer_grad = shift_back(inner_grad)
    spill = passed_along(extended_grad[:, : reach - 1], "seq", -1)
    keys_mixer_grad = extended_grad[:, reach - 1 :] + jnp.pad(
        spill, ((0, 0), (block_len - reach + 1, 0), (0, 0))
    )
    proj_grad_mixer = (
        jnp.concatenate([query_mixer_grad, keys_mixer_grad, value_mixer_grad], axis=2)
        .astype(bf16)
        .reshape(row_count, 3 * model_width)
    )
    into_normed_mixer, mixer_inputs_grad = dense_back(normed_low_mixer, w_mixer_in, proj_grad_mixer)
    into_start, mixer_gain_grad = back_mixer(into_normed_mixer)
    tokens_gradient = (upstream + into_start).reshape(seq_count, block_len, model_width).astype(bf16)

    small_rows = jnp.concatenate(
        [-jnp.exp(-decay) * power_grad, weight_grad * table_out, weight_grad * table_in, taps_grad.T]
        + [
            g[None]
            for g in (mixer_gain_grad, first_gain_grad, attend_gain_grad, second_gain_grad, skip_grad[0])
        ],
        axis=0,
    )
    small_grad = jnp.pad(small_rows, ((0, small_width - small_count), (0, 0))).T.astype(bf16)
    def unfolded(folded):
        return folded.reshape(share, fold, model_width).transpose(1, 0, 2).reshape(share * fold, model_width)

    gains_at = 3 * states + reach
    table_edges = [0, states, 2 * states, 3 * states, gains_at, small_width]

    def tables_of(block):
        return [block[:, a:b] for a, b in zip(table_edges, table_edges[1:])]

    last = [attend_inputs_grad, first_up_grad, mixer_output_grad, mixer_inputs_grad, small_grad]
    if by_kernel:
        last += [first_down_grad, attend_output_grad]
        orders = ("yxz", "xyz", "xzy", "yxz", "xyz", "yzx")
        plan = chunked([g.shape[1] for g in last], (6, 6, 2, 6, 2, 4, 2), orders)
        part = attend_cols // 3 // groups

        def finish(index, block, results):
            if index == 0:
                for group in range(groups):
                    for kind in range(3):
                        start = (kind * groups + group) * part
                        source = group * padded + kind * part
                        results[0][:, start : start + part] = block[:, source : source + part]
            elif index == 4:
                for place, table in enumerate(tables_of(block)):
                    results[5 + place][...] = table
            else:
                results[{1: 1, 2: 2, 3: 3, 5: 4, 6: 10}[index]][...] = block[...]

        widths = [attend_cols] + [g.shape[1] for g in last[1:4]]
        results = [shaped(share, w) for w in widths] + [shaped(share * fold, model_width)]
        results += [shaped(share, b - a) for a, b in zip(table_edges, table_edges[1:])]
        results.append(shaped(share, model_width))
        attend_inputs_out, first_up_out, mixer_output_out, mixer_inputs_out, first_down_out, *tables = (
            scatter_blocks(last, plan, finish, results, gap=4)
        )
        *tables, attend_output_out = tables
    else:
        last += [fold_all(first_down_grad, share, model_width), attend_output_grad]
        *last, folded, attend_output_out = scattered(last)
        first_down_out = unfolded(folded).astype(f32)
        grouped, first_up_out, mixer_output_out, mixer_inputs_out, small_out = (
            g.astype(f32) for g in last
        )
        attend_inputs_out = ungroup_columns(grouped, groups, padded, attend_cols)
        tables = tables_of(small_out)
    decay_out, in_out, out_out, taps_out, vectors = tables

    return (
        mixed,
        tokens_gradient,
        vectors[:, 0],
        mixer_inputs_out,
        taps_out,
        decay_out,
        in_out,
        out_out,
        vectors[:, 4],
        mixer_output_out,
        vectors[:, 1],
        first_up_out,
        first_down_out,
        vectors[:, 2],
        attend_inputs_out,
        attend_output_out.astype(f32),
        vectors[:, 3],
        second_up_out.astype(f32),
        unfolded(second_down_out).astype(f32),
    )


def solution(mesh):
    return jax.shard_map(
        body,
        mesh=mesh,
        in_specs=(
            P("batch", "seq", None),
            P("batch", "seq", None),
            P("batch"),
            P(("seq", "batch")),
            P(("seq", "batch"), None),
            P(("seq", "batch"), None),
            P(("seq", "batch"), None),
            P(("seq", "batch"), None),
            P(("seq", "batch"), None),
            P(("seq", "batch")),
            P(("seq", "batch"), None),
            P(("seq", "batch")),
            P(("seq", "batch"), None),
            P(("seq", "batch"), None),
            P(("seq", "batch")),
            P(("seq", "batch"), None),
            P(("seq", "batch"), None),
            P(("seq", "batch")),
            P(("seq", "batch"), None),
            P(("seq", "batch"), None),
        ),
        out_specs=(
            P("batch", "seq", None),
            P("batch", "seq", None),
            P(("seq", "batch")),
            P(("seq", "batch"), None),
            P(("seq", "batch"), None),
            P(("seq", "batch"), None),
            P(("seq", "batch"), None),
            P(("seq", "batch"), None),
            P(("seq", "batch")),
            P(("seq", "batch"), None),
            P(("seq", "batch")),
            P(("seq", "batch"), None),
            P(("seq", "batch"), None),
            P(("seq", "batch")),
            P(("seq", "batch"), None),
            P(("seq", "batch"), None),
            P(("seq", "batch")),
            P(("seq", "batch"), None),
            P(("seq", "batch"), None),
        ),
        check_vma=False,
    )
```

profile of v0, /device:TPU:0, one launch (start us, length us, event | category | flops | bytes accessed | tf_op | source)
XLA Modules:
  0.0 557.9 jit_solution(15029309000406775370)
XLA Ops:
  14.5 75.8 %shard_map.339 = (bf16[4,2,2,2,24,2560]{5,4,3,2,1,0:T(8,128)(2,1)}, bf16[4,2,2,2,96,768]{5,4,3,2,1,0:T(8,128)(2,1)}) custom-call(bf16[24,2560]{1,0:T(8,128)(2,1)} %fusion.22.refs_0_, bf16[96,768]{1,0:T(8,128)(2,1)} %refs_1_.1), custom_call_target="tpu_custom_call" | custom-call | bytes 17301504 | tf_op jit(solution)/shard_map/pallas_call | solution.py:305
  92.1 3.4 fusion
  100.5 29.4 %shard_map.340.carried_ref = f32[2,64,768]{2,1,0:T(8,128)} custom-call(f32[2,128,768]{2,1,0:T(8,128)} %get-tuple-element.161.input_ref, f32[64,768]{1,0:T(8,128)} %get-tuple-element.186.decay_ref), custom_call_target="tpu_custom_call" | custom-call | bytes 6291456 | tf_op jit(solution)/shard_map/pallas_call | solution.py:533
  132.1 9.3 %shard_map.341 = (f32[2,128,768]{2,1,0:T(8,128)S(1)}, f32[2,128,768]{2,1,0:T(8,128)S(1)}) custom-call(f32[2,128,768]{2,1,0:T(8,128)S(1)} %copy-done.2, f32[2,128,768]{2,1,0:T(8,128)S(1)} %get-tuple-element.163.query_ref, f32[2,64,768]{2,1,0:T(8,128)S(1)} %copy-done.7, f32[64,768]{1,0:T(8,128)S(1)} %copy-done.5, f32[64,768]{1,0:T(8,128)S(1)} %get-tuple-element.185.weight_ref, ...), custom_call_target="tpu_custom_call" | custom-call | bytes 2362368 | tf_op jit(solution)/shard_map/pallas_call | solution.py:154
  142.4 15.6 %all-gather.3.cloned.1.call-done.up_ref = bf16[768,10240]{1,0:T(8,128)(2,1)} async-done(((bf16[24,10240]{1,0:T(8,128)(2,1)}), bf16[768,10240]{1,0:T(8,128)(2,1)}) %all-gather.3.cloned.1.call-update) | async-done | bytes 15728656 | tf_op jit(solution)/shard_map/all_gather | solution.py:1188
  162.0 6.0 %shard_map.342 = (f32[256,768]{1,0:T(8,128)S(1)}, bf16[256,768]{1,0:T(8,128)(2,1)S(1)}, f32[256,3072]{1,0:T(8,128)S(1)}, bf16[256,3072]{1,0:T(8,128)(2,1)S(1)}) custom-call(f32[256,768]{1,0:T(8,128)S(1)} %convolution_add_fusion.1.resid_ref, f32[1,768]{1,0:T(1,128)S(1)} %get-tuple-element.183.gain_ref, ...), custom_call_target="tpu_custom_call" | custom-call | flops 2415919104 | bytes 23592960 | tf_op jit(solution)/shard_map/pallas_call | solution.py:572
  170.8 3.5 convolution_convert_fusion.2
  174.9 52.5 %all_to_all.20 = bf16[8,128,640]{2,1,0:T(8,128)(2,1)} all-to-all(bf16[8,128,640]{2,1,0:T(8,128)(2,1)S(1)} %bitcast.118), channel_id=1, replica_groups=mesh['seq'=8,'batch'=4] {'seq'}, dimensions={0} | all-to-all | bytes 2621440 | tf_op jit(solution)/shard_map/all_to_all | solution.py:1258
  227.3 11.0 %shard_map.343 = (bf16[1024,256]{1,0:T(8,128)(2,1)}, f32[1024,192]{1,0:T(8,128)}, f32[3,1024,128]{2,1,0:T(8,128)}) custom-call(bf16[1024,640]{1,0:T(8,128)(2,1)} %bitcast.113), custom_call_target="tpu_custom_call" | custom-call | tf_op jit(solution)/shard_map/pallas_call | solution.py:820
  238.4 4.1 all-to-all-start.1
  244.1 10.6 %all-to-all-done.1 = bf16[8,128,256]{2,1,0:T(8,128)(2,1)} async-done(((bf16[8,128,256]{2,1,0:T(8,128)(2,1)}), bf16[8,128,256]{2,1,0:T(8,128)(2,1)}, u32[]{:S(2)}, u32[]{:S(2)}) %all-to-all-start.1) | async-done | bytes 524320 | tf_op jit(solution)/shard_map/all_to_all | solution.py:1263
  260.4 6.1 %shard_map.344 = (f32[256,768]{1,0:T(8,128)S(1)}, bf16[256,768]{1,0:T(8,128)(2,1)S(1)}, f32[256,3072]{1,0:T(8,128)S(1)}, bf16[256,3072]{1,0:T(8,128)(2,1)S(1)}) custom-call(f32[256,768]{1,0:T(8,128)S(1)} %convolution_add_fusion.resid_ref, f32[1,768]{1,0:T(1,128)S(1)} %get-tuple-element.182.gain_ref, bf16[768,10240]{1,0:T(8,128)(2,1)} %all-gather.3.cloned.1.call-done.up_ref, ...), custom_call_target="tpu_custom_call" | custom-call | flops 2415919104 | bytes 23592960 | tf_op jit(solution)/shard_map/pallas_call | solution.py:572
  269.1 13.3 %shard_map.345 = (f32[256,768]{1,0:T(8,128)S(1)}, f32[1,768]{1,0:T(1,128)S(1)}, bf16[768,6144]{1,0:T(8,128)(2,1)}) custom-call(f32[256,768]{1,0:T(8,128)S(1)} %bitcast.110, f32[256,768]{1,0:T(8,128)S(1)} %convolution_add_fusion.resid_ref, f32[1,768]{1,0:T(1,128)S(1)} %get-tuple-element.182.gain_ref, bf16[256,768]{1,0:T(8,128)(2,1)S(1)} %get-tuple-element.68.normed_ref, ...), custom_call_target="tpu_custom_call" | custom-call | flops 4831838208 | bytes 37748736 | tf_op jit(solution)/shard_map/pallas_call | solution.py:709
  283.1 16.9 %all_to_all.21 = bf16[8,128,256]{2,1,0:T(8,128)(2,1)} all-to-all(bf16[8,128,256]{2,1,0:T(8,128)(2,1)S(1)} %bitcast.129), channel_id=1, replica_groups=mesh['seq'=8,'batch'=4] {'seq'}, dimensions={0} | all-to-all | bytes 1048576 | tf_op jit(solution)/shard_map/all_to_all | solution.py:1258
  300.0 12.4 %shard_map.346 = bf16[1024,640]{1,0:T(8,128)(2,1)} custom-call(bf16[1024,640]{1,0:T(8,128)(2,1)} %bitcast.114, bf16[1024,256]{1,0:T(8,128)(2,1)} %bitcast.131, f32[1024,192]{1,0:T(8,128)} %get-tuple-element.72.full_ref, f32[3,1024,128]{2,1,0:T(8,128)} %get-tuple-element.73.stat_ref), custom_call_target="tpu_custom_call" | custom-call | tf_op jit(solution)/shard_map/pallas_call | solution.py:837
  312.5 4.6 all-to-all-start.3
  318.9 28.8 %all-to-all-done.3 = bf16[8,128,640]{2,1,0:T(8,128)(2,1)} async-done(((bf16[8,128,640]{2,1,0:T(8,128)(2,1)}), bf16[8,128,640]{2,1,0:T(8,128)(2,1)}, u32[]{:S(2)}, u32[]{:S(2)}) %all-to-all-start.3) | async-done | bytes 1310752 | tf_op jit(solution)/shard_map/all_to_all | solution.py:1263
  349.3 4.1 multiply_reduce_fusion
  354.9 12.7 %shard_map.347 = (f32[256,768]{1,0:T(8,128)S(1)}, f32[1,768]{1,0:T(1,128)S(1)}, bf16[768,3072]{1,0:T(8,128)(2,1)}, bf16[3072,768]{1,0:T(8,128)(2,1)}) custom-call(f32[256,768]{1,0:T(8,128)S(1)} %add_add_fusion.2.upstream_ref, f32[256,768]{1,0:T(8,128)S(1)} %convolution_add_fusion.1.resid_ref, f32[1,768]{1,0:T(1,128)S(1)} %get-tuple-element.183.gain_ref, ...), custom_call_target="tpu_custom_call" | custom-call | flops 4831838208 | bytes 37748736 | tf_op jit(solution)/shard_map/pallas_call | solution.py:709
  371.9 22.0 %shard_map.348.later_ref = f32[2,64,768]{2,1,0:T(8,128)} custom-call(f32[2,128,768]{2,1,0:T(8,128)} %get-tuple-element.176.input_ref.grad_ref, f32[64,768]{1,0:T(8,128)} %get-tuple-element.186.decay_ref), custom_call_target="tpu_custom_call" | custom-call | bytes 6291456 | tf_op jit(solution)/shard_map/pallas_call | solution.py:533
  396.1 20.8 %shard_map.349 = (f32[2,128,768]{2,1,0:T(8,128)S(1)}, f32[64,768]{1,0:T(8,128)S(1)}, f32[64,768]{1,0:T(8,128)S(1)}, f32[1,768]{1,0:T(1,128)S(1)}) custom-call(f32[2,128,768]{2,1,0:T(8,128)S(1)} %copy-done.3, f32[2,128,768]{2,1,0:T(8,128)S(1)} %copy-done.4, f32[2,64,768]{2,1,0:T(8,128)S(1)} %copy-done.8, f32[2,64,768]{2,1,0:T(8,128)S(1)} %copy-done.13, ...), custom_call_target="tpu_custom_call" | custom-call | bytes 2755584 | tf_op jit(solution)/shard_map/pallas_call | solution.py:154
  424.0 3.3 convolution_convert_fusion.1
  431.5 2.9 convolution_convert_fusion
  434.4 103.8 %shard_map.350 = (f32[24,2304]{1,0:T(8,128)}, f32[24,3072]{1,0:T(8,128)}, f32[24,768]{1,0:T(8,128)}, f32[24,2304]{1,0:T(8,128)}, f32[96,768]{1,0:T(8,128)}, /*in...) custom-call(bf16[4,2,2,2,24,2560]{5,4,3,2,1,0:T(8,128)(2,1)} %bitcas, ...), custom_call_target="tpu_custom_call" | custom-call | bytes 78643200 | tf_op jit(solution)/shard_map/pallas_call | solution.py:444
  (266 shorter events, 69.4 us)
Async XLA Ops:
  7.3 150.6 %all-gather.3.cloned.1.call-start = ((), (), s32[]{:S(2)}) async-start(), calls=%async_computation.5 | async-start | bytes 16220160 | tf_op jit(solution)/shard_map/all_gather | solution.py:1188
  8.7 82.9 %copy-start.18 = (bf16[2,128,768]{2,1,0:T(8,128)(2,1)S(1)}, bf16[2,128,768]{2,1,0:T(8,128)(2,1)}, u32[]{:S(2)}) copy-start(bf16[2,128,768]{2,1,0:T(8,128)(2,1)} %param.20) | copy-start | bytes 1179652
  13.1 244.9 %all-gather.5.cloned.1.call-start = ((), (), s32[]{:S(2)}) async-start(), calls=%async_computation.6 | async-start | bytes 4866048 | tf_op jit(solution)/shard_map/all_gather | solution.py:1194
  95.6 3.4 collective-permute-start
  98.9 30.9 %copy-start.5 = (f32[64,768]{1,0:T(8,128)S(1)}, f32[64,768]{1,0:T(8,128)}, u32[]{:S(2)}) copy-start(f32[64,768]{1,0:T(8,128)} %get-tuple-element.186.decay_ref) | copy-start | bytes 589828
  142.3 17.3 %copy-start.26 = (bf16[2,128,768]{2,1,0:T(8,128)(2,1)}, bf16[2,128,768]{2,1,0:T(8,128)(2,1)S(1)}, u32[]{:S(2)}) copy-start(bf16[2,128,768]{2,1,0:T(8,128)(2,1)S(1)} %convert_element_type.109) | copy-start | bytes 1179652
  174.9 67.9 %copy-start.70 = (s32[2]{0:T(128)S(1)}, s32[2]{0:T(128)}, u32[]{:S(2)}) copy-start(s32[2]{0:T(128)} %param.22) | copy-start | bytes 28
  227.3 15.5 %slice-start = ((bf16[768,10240]{1,0:T(8,128)(2,1)}), bf16[768,768]{1,0:T(8,128)(2,1)S(1)}, s32[]{:S(2)}) async-start(bf16[768,10240]{1,0:T(8,128)(2,1)} %all-gather.3.cloned.1.call-done.up_ref), calls=%async_computation.8 | async-start | bytes 2359296 | tf_op jit(solution)/shard_map/slice | solution.py:1116
  238.4 16.4 %all-to-all-start.1 = ((bf16[8,128,256]{2,1,0:T(8,128)(2,1)}), bf16[8,128,256]{2,1,0:T(8,128)(2,1)}, u32[]{:S(2)}, u32[]{:S(2)}) async-start(bf16[8,128,256]{2,1,0:T(8,128)(2,1)} %bitcast.137), calls=%async_computation.1 | async-start | bytes 1048576 | tf_op jit(solution)/shard_map/all_to_all | solution.py:1263
  242.5 298.9 %reduce-scatter.2.cloned.1.call-start = ((), (), s32[]{:S(2)}) async-start(), calls=%async_computation.7 | async-start | bytes 9732096 | tf_op jit(solution)/shard_map/reduce_scatter | solution.py:1314
  269.1 13.3 %copy-start.23 = (bf16[4,256,768]{2,1,0:T(8,128)(2,1)S(1)}, bf16[4,256,768]{2,1,0:T(8,128)(2,1)}, u32[]{:S(2)}) copy-start(bf16[4,256,768]{2,1,0:T(8,128)(2,1)} %pad.47) | copy-start | bytes 4718596
  312.5 35.2 %all-to-all-start.3 = ((bf16[8,128,640]{2,1,0:T(8,128)(2,1)}), bf16[8,128,640]{2,1,0:T(8,128)(2,1)}, u32[]{:S(2)}, u32[]{:S(2)}) async-start(bf16[8,128,640]{2,1,0:T(8,128)(2,1)} %bitcast.119), calls=%async_computation.3 | async-start | bytes 2621440 | tf_op jit(solution)/shard_map/all_to_all | solution.py:1263
  317.8 31.4 %copy-start.68 = (f32[256]{0:T(256)S(1)}, f32[256]{0:T(256)}, u32[]{:S(2)}) copy-start(f32[256]{0:T(256)} %copy-done.67) | copy-start | bytes 3076
  369.4 24.5 %copy-start.3 = (f32[2,128,768]{2,1,0:T(8,128)S(1)}, f32[2,128,768]{2,1,0:T(8,128)}, u32[]{:S(2)}) copy-start(f32[2,128,768]{2,1,0:T(8,128)} %get-tuple-element.161.input_ref) | copy-start | bytes 2359300
  369.4 24.5 %copy-start.6 = (f32[64,768]{1,0:T(8,128)S(1)}, f32[64,768]{1,0:T(8,128)}, u32[]{:S(2)}) copy-start(f32[64,768]{1,0:T(8,128)} %get-tuple-element.186.decay_ref) | copy-start | bytes 589828
  369.5 24.5 %copy-start.8 = (f32[2,64,768]{2,1,0:T(8,128)S(1)}, f32[2,64,768]{2,1,0:T(8,128)}, u32[]{:S(2)}) copy-start(f32[2,64,768]{2,1,0:T(8,128)} %shard_map.340.carried_ref) | copy-start | bytes 1179652
  396.1 20.8 %copy-start.21 = (f32[2,128,2304]{2,1,0:T(8,128)S(1)}, f32[2,128,2304]{2,1,0:T(8,128)}, u32[]{:S(2)}) copy-start(f32[2,128,2304]{2,1,0:T(8,128)} %copy-done.20) | copy-start | bytes 7077892
  419.7 7.6 %collective-permute-start.1 = (f32[2,3,768]{2,1,0:T(4,128)S(1)}, f32[2,3,768]{2,1,0:T(4,128)S(1)}, u32[]{:S(2)}, u32[]{:S(2)}) collective-permute-start(f32[2,3,768]{2,1,0:T(4,128)S(1)} %pad_add_fusion.1), channel_id=1, source_target_pairs={{4,0},{8,4},{12,8},{16,12},{20,16},{24,20},{28,24},{5,1},{9,5},{13... | collective-permute-start | bytes 55304 | tf_op jit(solution)/shard_map/ppermute | solution.py:183
  538.2 8.7 %copy-start.59 = (f32[24,64]{1,0:T(8,128)S(1)}, f32[24,64]{1,0:T(8,128)}, u32[]{:S(2)}) copy-start(f32[24,64]{1,0:T(8,128)} %get-tuple-element.234) | copy-start | bytes 18436
  538.2 9.3 %copy-start.57 = (f32[24,768]{1,0:T(8,128)S(1)}, f32[24,768]{1,0:T(8,128)}, u32[]{:S(2)}) copy-start(f32[24,768]{1,0:T(8,128)} %get-tuple-element.236) | copy-start | bytes 221188
  538.2 9.9 %copy-start.47 = (f32[24,3072]{1,0:T(8,128)S(1)}, f32[24,3072]{1,0:T(8,128)}, u32[]{:S(2)}) copy-start(f32[24,3072]{1,0:T(8,128)} %get-tuple-element.238) | copy-start | bytes 884740
  538.3 10.6 %copy-start.46 = (f32[96,768]{1,0:T(8,128)S(1)}, f32[96,768]{1,0:T(8,128)}, u32[]{:S(2)}) copy-start(f32[96,768]{1,0:T(8,128)} %get-tuple-element.239) | copy-start | bytes 884740
  538.3 11.3 %copy-start.48 = (f32[24,2304]{1,0:T(8,128)S(1)}, f32[24,2304]{1,0:T(8,128)}, u32[]{:S(2)}) copy-start(f32[24,2304]{1,0:T(8,128)} %get-tuple-element.241) | copy-start | bytes 663556
  538.3 12.0 %copy-start.56 = (f32[24,768]{1,0:T(8,128)S(1)}, f32[24,768]{1,0:T(8,128)}, u32[]{:S(2)}) copy-start(f32[24,768]{1,0:T(8,128)} %get-tuple-element.242) | copy-start | bytes 221188
  (60 other events, 210.4 us)
Sparse Core Ops, SparseCore 0:
  13.2 144.6 all-gather.2
  160.8 69.8 all-gather.4
  312.6 146.6 reduce-scatter.1
where the time goes:
time: 567 us; the launch traced here: 558 us
  Pallas kernels  323 us (57%)
  blocking collectives  69.4 us (12%)
  waiting for transfers between devices  55.7 us (10%)
  local copies, waits for them, and re-layouts  40.2 us (7%)
  matrix products  26.8 us (5%)
  between operations  15.6 us (3%)
  other arithmetic  15 us (3%)
  starting transfers between devices  12.6 us (2%)
    pallas_call x1, Pallas kernels, scatter_blocks(): pl.pallas_call(functools.partial(scatter_kernel, plan, gap, finish, (len(...  104 us
    pallas_call x1, Pallas kernels, gather_blocks(): pl.pallas_call(functools.partial(gather_kernel, plan, gap), out_shape=out...  75.8 us
    all_to_all x2, blocking collectives, deal(): lax.all_to_all(parts, 'seq', split_axis=0, concat_axis=0, tiled=True)  69.4 us
    pallas_call x2, Pallas kernels, carried_by_kernel(): pl.pallas_call(functools.partial(carry_kernel, reverse), out_shape=shaped...  51.5 us
    all_to_all x2, waiting for transfers between devices, collect(): back = lax.all_to_all(parts, 'seq', split_axis=0, concat_axis=0, tiled=True)  39.4 us
    pallas_call x2, Pallas kernels, per_lane_tile(): pl.pallas_call(kernel, grid=(args[0].shape[-1] // lanes,), in_specs=[spec...  30.1 us
    unnamed x169, local copies, waits for them, and re-layouts  27.9 us
    pallas_call x2, Pallas kernels, feed_back_blocks(): pl.pallas_call(functools.partial(feed_back_kernel, packed), grid=(inner /...  25.9 us
  transfers between devices with their start and end apart: 7, of which 4 were waited for; matrix products, arithmetic and copies ran while one was open for 9% of the time, Pallas kernels for 52%

commit v1 on v0

--- a/solution.py
+++ b/solution.py
@@ -362,11 +362,10 @@
             started[chunk, 0].wait_recv()
             loads[chunk].wait()
 
-            @pl.loop(0, box[0])
-            def _(row):
-                for i in range(2):
-                    for j in range(2):
-                        held[row, i, j] = add_into(held[row, i, j], from_core[row, i, j])
+            @pl.loop(0, 4 * box[0])
+            def _(turn):
+                at = (lax.div(turn, 4), lax.rem(lax.div(turn, 2), 2), lax.rem(turn, 2))
+                held[at] = add_into(held[at], from_core[at])
 
             if x_first:
                 push(chunk, 1, held.at[:, :, 1 - y], from_one, to_y)
@@ -375,13 +374,11 @@
         elif stage == 1:
             started[chunk, 1].wait_recv()
 
-            @pl.loop(0, box[0])
-            def _(row):
-                for i in range(2):
-                    if x_first:
-                        held[row, i, y] = add_into(held[row, i, y], from_one[row, i])
-                    else:
-                        held[row, x, i] = add_into(held[row, x, i], from_one[row, i])
+            @pl.loop(0, 2 * box[0])
+            def _(turn):
+                row, i = lax.div(turn, 2), lax.rem(turn, 2)
+                at = (row, i, y) if x_first else (row, x, i)
+                held[at] = add_into(held[at], from_one[row, i])
 
             if not line_last:
                 for step in range(1, box[0]):
@@ -482,13 +479,15 @@
         peer = (lax.rem(me + step, count), batch)
         pl.semaphore_signal(barrier, inc=1, device_id=peer, device_id_type=MESH)
 
-    for tile in range(width // lanes):
-        columns = slice(tile * lanes, (tile + 1) * lanes)
+    @pl.loop(0, width // lanes)
+    def _(tile):
+        columns = pl.ds(pl.multiple_of(tile * lanes, lanes), lanes)
         encode_kernel(reverse, input_ref.at[:, :, columns], decay_ref.at[:, columns], ends)
         for group in range(count):
             rows = slice(group * part, (group + 1) * part)
             mine = jnp.concatenate([ends[seq, rows] for seq in range(seq_count)], axis=0)
             outgoing[group, :, columns] = mine.astype(bf16)
+
     pl.semaphore_wait(barrier, count - 1)
 
     def exchange(phase, source, target):
@@ -543,7 +542,7 @@
     )(value, decay)
 
 
-hidden_block = 768
+hidden_block = 384
 gelu_scale = 0.7978845608
 gelu_cubic = 0.044715
 
@@ -588,7 +587,7 @@
         cost_estimate=pl.CostEstimate(
             flops=4 * rows * width * inner, bytes_accessed=10 * width * inner, transcendentals=rows * inner
         ),
-        compiler_params=pltpu.CompilerParams(vmem_limit_bytes=40 * 1024 * 1024),
+        compiler_params=pltpu.CompilerParams(vmem_limit_bytes=60 * 1024 * 1024),
     )(resid, gain[None], up_packed, down)
     return out, (resid, gain, normed, hidden, active)
 
@@ -725,16 +724,17 @@
         cost_estimate=pl.CostEstimate(
             flops=8 * rows * width * inner, bytes_accessed=16 * width * inner, transcendentals=rows * inner
         ),
-        compiler_params=pltpu.CompilerParams(vmem_limit_bytes=48 * 1024 * 1024),
+        compiler_params=pltpu.CompilerParams(vmem_limit_bytes=60 * 1024 * 1024),
     )(upstream, resid, gain[None], normed, hidden, active, up_packed, down)
     return (out, gain_grad[0], *grads)
 
 
-def split_heads(ref, scratch, heads, parts, first=0):
-    for part in range(parts):
-        for head in range(heads):
-            start = (part * heads + head) * HEAD_DIM + first
-            scratch[part * heads + head] = ref[:, start : start + HEAD_DIM]
+def split_heads(ref, scratch, heads, parts):
+    @pl.loop(0, ref.shape[0] // lanes)
+    def _(turn):
+        rows = pl.ds(pl.multiple_of(turn * lanes, lanes), lanes)
+        for part in range(parts * heads):
+            scratch[part, rows, :] = ref[rows, part * HEAD_DIM : (part + 1) * HEAD_DIM]
 
 
 def score_block(query, keys, first, scale):
@@ -746,31 +746,48 @@
     return jnp.where(columns <= rows, scores, masked_score)
 
 
+def over_blocks(one_block, heads, length, block):
+    span = min(2 * block, length)
+
+    @pl.loop(0, heads)
+    def _(head):
+        for start in range(0, length, span):
+
+            @pl.loop(0, span // block)
+            def _(half):
+                one_block(head, pl.multiple_of(start + half * block, block), start + span)
+
+
 def attend_kernel(heads, block, scale, qkv_ref, low_ref, full_ref, stat_ref, parts, outs):
     length = qkv_ref.shape[0]
     split_heads(qkv_ref, parts, heads, 3)
 
-    @pl.loop(0, heads)
-    def _(head):
-        for first in range(0, length, block):
-            extent = first + block
-            query = parts[head, first:extent, :]
-            scores = score_block(query, parts[heads + head, :extent, :], first, scale)
-            top = jnp.max(scores, axis=1, keepdims=True)
-            soft = jnp.exp(scores - top)
-            whole = jnp.sum(soft, axis=1, keepdims=True)
-            soft = soft * (1.0 / whole)
-            outs[head, first:extent, :] = jnp.dot(
-                soft.astype(bf16), parts[2 * heads + head, :extent, :], preferred_element_type=f32
-            )
-            stat_ref[head, first:extent, :] = jnp.broadcast_to(top + jnp.log(whole), (block, lanes))
-
-    if low_ref.shape[1] > heads * HEAD_DIM:
-        low_ref[:, heads * HEAD_DIM :] = jnp.zeros((length, low_ref.shape[1] - heads * HEAD_DIM), bf16)
-    for head in range(heads):
-        place = slice(head * HEAD_DIM, (head + 1) * HEAD_DIM)
-        full_ref[:, place] = outs[head]
-        low_ref[:, place] = outs[head].astype(bf16)
+    def one_block(head, first, extent):
+        here_rows = pl.ds(first, block)
+        query = parts[head, here_rows, :]
+        scores = score_block(query, parts[heads + head, :extent, :], first, scale)
+        top = jnp.max(scores, axis=1, keepdims=True)
+        soft = jnp.exp(scores - top)
+        whole = jnp.sum(soft, axis=1, keepdims=True)
+        soft = soft * (1.0 / whole)
+        outs[head, here_rows, :] = jnp.dot(
+            soft.astype(bf16), parts[2 * heads + head, :extent, :], preferred_element_type=f32
+        )
+        stat_ref[head, here_rows, :] = jnp.broadcast_to(top + jnp.log(whole), (block, lanes))
+
+    over_blocks(one_block, heads, length, block)
+
+    @pl.loop(0, length // lanes)
+    def _(turn):
+        rows = pl.ds(pl.multiple_of(turn * lanes, lanes), lanes)
+        if low_ref.shape[1] > heads * HEAD_DIM:
+            rest = low_ref.shape[1] - heads * HEAD_DIM
+            low_ref[rows, heads * HEAD_DIM :] = jnp.zeros((lanes, rest), bf16)
+        for head in range(heads):
+            place = slice(head * HEAD_DIM, (head + 1) * HEAD_DIM)
+            found = outs[head, rows, :]
+            full_ref[rows, place] = found
+            low_ref[rows, place] = found.astype(bf16)
 
 
 def attend_back_kernel(
@@ -780,34 +797,42 @@
     split_heads(qkv_ref, parts, heads, 3)
     split_heads(dout_ref, douts, heads, 1)
     split_heads(full_ref, fulls, heads, 1)
-    grads[...] = jnp.zeros_like(grads)
-
-    @pl.loop(0, heads)
-    def _(head):
-        for first in range(0, length, block):
-            extent = first + block
-            query = parts[head, first:extent, :]
-            keys = parts[heads + head, :extent, :]
-            value = parts[2 * heads + head, :extent, :]
-            dout = douts[head, first:extent, :]
-            delta = jnp.sum(dout.astype(f32) * fulls[head, first:extent, :], axis=1, keepdims=True)
-            scores = score_block(query, keys, first, scale)
-            soft = jnp.exp(scores - stat_ref[head, first:extent, :1])
-            across = (((1,), (1,)), ((), ()))
-            along = (((0,), (0,)), ((), ()))
-            dprob = lax.dot_general(dout, value, across, preferred_element_type=f32)
-            dscore = (soft * (dprob - delta) * scale).astype(bf16)
-            grads[head, first:extent, :] = jnp.dot(dscore, keys, preferred_element_type=f32)
-            grads[heads + head, :extent, :] += lax.dot_general(
-                dscore, query, along, preferred_element_type=f32
-            )
-            grads[2 * heads + head, :extent, :] += lax.dot_general(
-                soft.astype(bf16), dout, along, preferred_element_type=f32
-            )
-
-    grad_ref[...] = jnp.zeros_like(grad_ref)
-    for part in range(3 * heads):
-        grad_ref[:, part * HEAD_DIM : (part + 1) * HEAD_DIM] = grads[part].astype(bf16)
+
+    @pl.loop(0, 3 * heads)
+    def _(part):
+        grads[part] = jnp.zeros(grads.shape[1:], f32)
+
+    def one_block(head, first, extent):
+        here_rows = pl.ds(first, block)
+        query = parts[head, here_rows, :]
+        keys = parts[heads + head, :extent, :]
+        value = parts[2 * heads + head, :extent, :]
+        dout = douts[head, here_rows, :]
+        delta = jnp.sum(dout.astype(f32) * fulls[head, here_rows, :], axis=1, keepdims=True)
+        scores = score_block(query, keys, first, scale)
+        soft = jnp.exp(scores - stat_ref[head, here_rows, :1])
+        across = (((1,), (1,)), ((), ()))
+        along = (((0,), (0,)), ((), ()))
+        dprob = lax.dot_general(dout, value, across, preferred_element_type=f32)
+        dscore = (soft * (dprob - delta) * scale).astype(bf16)
+        grads[head, here_rows, :] = jnp.dot(dscore, keys, preferred_element_type=f32)
+        grads[heads + head, :extent, :] += lax.dot_general(
+            dscore, query, along, preferred_element_type=f32
+        )
+        grads[2 * heads + head, :extent, :] += lax.dot_general(
+            soft.astype(bf16), dout, along, preferred_element_type=f32
+        )
+
+    over_blocks(one_block, heads, length, block)
+
+    @pl.loop(0, length // lanes)
+    def _(turn):
+        rows = pl.ds(pl.multiple_of(turn * lanes, lanes), lanes)
+        rest = grad_ref.shape[1] - 3 * heads * HEAD_DIM
+        if rest:
+            grad_ref[rows, 3 * heads * HEAD_DIM :] = jnp.zeros((lanes, rest), bf16)
+        for part in range(3 * heads):
+            grad_ref[rows, part * HEAD_DIM : (part + 1) * HEAD_DIM] = grads[part, rows, :].astype(bf16)
 
 
 def attend_params():
@@ -1249,7 +1274,7 @@
     proj_low = dense(normed_low_attend, w_attend_in).astype(bf16)
     if dealt:
         length = seq_devices * block_len
-        block = min(256, length)
+        block = min(128, length)
 
         def deal(array, width):
             array = array.reshape(seq_count, block_len, groups * width)
@@ -1375,7 +1400,7 @@
     if by_kernel:
         last += [first_down_grad, attend_output_grad]
         orders = ("yxz", "xyz", "xzy", "yxz", "xyz", "yzx")
-        plan = chunked([g.shape[1] for g in last], (6, 6, 2, 6, 2, 4, 2), orders)
+        plan = chunked([g.shape[1] for g in last], (4, 4, 2, 4, 2, 4, 2), orders)
         part = attend_cols // 3 // groups
 
         def finish(index, block, results):

time: 567 us -> 591 us (1.042); the launches traced: 558 us -> 588 us
  Pallas kernels: 323 us -> 348 us
  local copies, waits for them, and re-layouts: 40.2 us -> 30.8 us
    unnamed x169 -> x171, local copies, waits for them, and re-layouts: 27.9 us -> 17.9 us
    pallas_call x2, Pallas kernels: 25.9 us -> 35.6 us  [feed_back_blocks(): pl.pallas_call(functools.partial(feed_back_kernel, packed), grid=(inner /...]
    pallas_call x2, Pallas kernels: 12 us -> 20.7 us  [feed_forward_blocks(): pl.pallas_call(feed_kernel, grid=(inner // hidden_block,), in_specs=[whol...]
    pallas_call x1, Pallas kernels: 12.4 us -> 20 us  [attend_whole_back(): pl.pallas_call(functools.partial(attend_back_kernel, heads, block, HEAD_D...]
    pallas_call x1, Pallas kernels: 11 us -> 18 us  [attend_whole(): pl.pallas_call(functools.partial(attend_kernel, heads, block, HEAD_DIM **...]
  transfers between devices with their start and end apart: 7 -> 7, of which waited for: 4 -> 4; matrix products, arithmetic and copies ran while one was open for 9% -> 10% of each run, Pallas kernels for 52% -> 51%
where the time goes in v1:
time: 591 us; the launch traced here: 588 us
  Pallas kernels  348 us (59%)
  blocking collectives  72 us (12%)
  waiting for transfers between devices  57.9 us (10%)
  matrix products  31.1 us (5%)
  local copies, waits for them, and re-layouts  30.8 us (5%)
  other arithmetic  20.5 us (3%)
  between operations  15.2 us (3%)
  starting transfers between devices  12.6 us (2%)
    pallas_call x1, Pallas kernels, scatter_blocks(): pl.pallas_call(functools.partial(scatter_kernel, plan, gap, finish, (len(...  98.4 us
    pallas_call x1, Pallas kernels, gather_blocks(): pl.pallas_call(functools.partial(gather_kernel, plan, gap), out_shape=out...  75.8 us
    all_to_all x2, blocking collectives, deal(): lax.all_to_all(parts, 'seq', split_axis=0, concat_axis=0, tiled=True)  72 us
    pallas_call x2, Pallas kernels, carried_by_kernel(): pl.pallas_call(functools.partial(carry_kernel, reverse), out_shape=shaped...  49.6 us
    all_to_all x2, waiting for transfers between devices, collect(): back = lax.all_to_all(parts, 'seq', split_axis=0, concat_axis=0, tiled=True)  40.3 us
    pallas_call x2, Pallas kernels, feed_back_blocks(): pl.pallas_call(functools.partial(feed_back_kernel, packed), grid=(inner /...  35.6 us
    pallas_call x2, Pallas kernels, per_lane_tile(): pl.pallas_call(kernel, grid=(args[0].shape[-1] // lanes,), in_specs=[spec...  30.1 us
    pallas_call x2, Pallas kernels, feed_forward_blocks(): pl.pallas_call(feed_kernel, grid=(inner // hidden_block,), in_specs=[whol...  20.7 us
  transfers between devices with their start and end apart: 7, of which 4 were waited for; matrix products, arithmetic and copies ran while one was open for 10% of the time, Pallas kernels for 51%

profile of v1, /device:TPU:0, one launch (start us, length us, event | category | flops | bytes accessed | tf_op | source)
XLA Modules:
  0.0 588.2 jit_solution(13200945876931389728)
XLA Ops:
  14.5 75.8 %shard_map.339 = (bf16[4,2,2,2,24,2560]{5,4,3,2,1,0:T(8,128)(2,1)}, bf16[4,2,2,2,96,768]{5,4,3,2,1,0:T(8,128)(2,1)}) custom-call(bf16[24,2560]{1,0:T(8,128)(2,1)} %fusion.22.refs_0_, bf16[96,768]{1,0:T(8,128)(2,1)} %refs_1_.1), custom_call_target="tpu_custom_call" | custom-call | bytes 17301504 | tf_op jit(solution)/shard_map/pallas_call | solution.py:305
  93.3 3.2 fusion
  101.4 28.0 %shard_map.340.carried_ref = f32[2,64,768]{2,1,0:T(8,128)} custom-call(f32[2,128,768]{2,1,0:T(8,128)} %get-tuple-element.161.input_ref, f32[64,768]{1,0:T(8,128)} %get-tuple-element.186.decay_ref), custom_call_target="tpu_custom_call" | custom-call | bytes 6291456 | tf_op jit(solution)/shard_map/pallas_call | solution.py:532
  131.5 9.3 %shard_map.341 = (f32[2,128,768]{2,1,0:T(8,128)S(1)}, f32[2,128,768]{2,1,0:T(8,128)S(1)}) custom-call(f32[2,128,768]{2,1,0:T(8,128)S(1)} %copy-done, f32[2,128,768]{2,1,0:T(8,128)S(1)} %get-tuple-element.163.query_ref, f32[2,64,768]{2,1,0:T(8,128)S(1)} %copy-done.5, f32[64,768]{1,0:T(8,128)S(1)} %copy-done.3, f32[64,768]{1,0:T(8,128)S(1)} %get-tuple-element.185.weight_ref, ...), custom_call_target="tpu_custom_call" | custom-call | bytes 2362368 | tf_op jit(solution)/shard_map/pallas_call | solution.py:154
  140.9 16.9 %all-gather.3.cloned.1.call-done.up_ref = bf16[768,10240]{1,0:T(8,128)(2,1)} async-done(((bf16[24,10240]{1,0:T(8,128)(2,1)}), bf16[768,10240]{1,0:T(8,128)(2,1)}) %all-gather.3.cloned.1.call-update) | async-done | bytes 15728656 | tf_op jit(solution)/shard_map/all_gather | solution.py:1213
  160.5 10.4 %shard_map.342 = (f32[256,768]{1,0:T(8,128)}, bf16[256,768]{1,0:T(8,128)(2,1)}, f32[256,3072]{1,0:T(8,128)}, bf16[256,3072]{1,0:T(8,128)(2,1)}) custom-call(f32[256,768]{1,0:T(8,128)} %convolution_add_fusion.1.resid_ref, f32[1,768]{1,0:T(1,128)} %get-tuple-element.183.gain_ref, bf16[768,10240]{1,0:T(8,128)(2,1)} %all-gather.3.cloned.1.call-done.up_ref, ...), custom_call_target="tpu_custom_call" | custom-call | flops 2415919104 | bytes 23592960 | tf_op jit(solution)/shard_map/pallas_call | solution.py:571
  173.5 3.6 convolution_convert_fusion.2
  177.6 54.3 %all_to_all.20 = bf16[8,128,640]{2,1,0:T(8,128)(2,1)} all-to-all(bf16[8,128,640]{2,1,0:T(8,128)(2,1)S(1)} %bitcast.116), channel_id=1, replica_groups=mesh['seq'=8,'batch'=4] {'seq'}, dimensions={0} | all-to-all | bytes 2621440 | tf_op jit(solution)/shard_map/all_to_all | solution.py:1283
  231.9 18.0 %shard_map.343 = (bf16[1024,256]{1,0:T(8,128)(2,1)}, f32[1024,192]{1,0:T(8,128)}, f32[3,1024,128]{2,1,0:T(8,128)}) custom-call(bf16[1024,640]{1,0:T(8,128)(2,1)} %bitcast.111), custom_call_target="tpu_custom_call" | custom-call | tf_op jit(solution)/shard_map/pallas_call | solution.py:845
  249.9 4.1 all-to-all-start.1
  255.7 12.3 %all-to-all-done.1 = bf16[8,128,256]{2,1,0:T(8,128)(2,1)} async-done(((bf16[8,128,256]{2,1,0:T(8,128)(2,1)}), bf16[8,128,256]{2,1,0:T(8,128)(2,1)}, u32[]{:S(2)}, u32[]{:S(2)}) %all-to-all-start.1) | async-done | bytes 524320 | tf_op jit(solution)/shard_map/all_to_all | solution.py:1288
  269.1 3.2 convolution_add_fusion.resid_ref
  272.2 10.4 %shard_map.344 = (f32[256,768]{1,0:T(8,128)}, bf16[256,768]{1,0:T(8,128)(2,1)}, f32[256,3072]{1,0:T(8,128)}, bf16[256,3072]{1,0:T(8,128)(2,1)}) custom-call(f32[256,768]{1,0:T(8,128)} %convolution_add_fusion.resid_ref, f32[1,768]{1,0:T(1,128)} %get-tuple-element.182.gain_ref, bf16[768,10240]{1,0:T(8,128)(2,1)} %all-gather.3.cloned.1.call-done.up_ref, ...), custom_call_target="tpu_custom_call" | custom-call | flops 2415919104 | bytes 23592960 | tf_op jit(solution)/shard_map/pallas_call | solution.py:571
  284.9 18.1 %shard_map.345 = (f32[256,768]{1,0:T(8,128)}, f32[1,768]{1,0:T(1,128)}, bf16[768,6144]{1,0:T(8,128)(2,1)}) custom-call(f32[256,768]{1,0:T(8,128)} %bitcast.125, f32[256,768]{1,0:T(8,128)} %convolution_add_fusion.resid_ref, f32[1,768]{1,0:T(1,128)} %get-tuple-element.182.gain_ref, bf16[256,768]{1,0:T(8,128)(2,1)} %get-tuple-element.68.normed_ref, ...), custom_call_target="tpu_custom_call" | custom-call | flops 4831838208 | bytes 37748736 | tf_op jit(solution)/shard_map/pallas_call | solution.py:708
  305.5 17.7 %all_to_all.21 = bf16[8,128,256]{2,1,0:T(8,128)(2,1)} all-to-all(bf16[8,128,256]{2,1,0:T(8,128)(2,1)S(1)} %bitcast.127), channel_id=1, replica_groups=mesh['seq'=8,'batch'=4] {'seq'}, dimensions={0} | all-to-all | bytes 1048576 | tf_op jit(solution)/shard_map/all_to_all | solution.py:1283
  323.2 20.0 %shard_map.346 = bf16[1024,640]{1,0:T(8,128)(2,1)} custom-call(bf16[1024,640]{1,0:T(8,128)(2,1)} %bitcast.112, bf16[1024,256]{1,0:T(8,128)(2,1)} %bitcast.129, f32[1024,192]{1,0:T(8,128)} %get-tuple-element.72.full_ref, f32[3,1024,128]{2,1,0:T(8,128)} %get-tuple-element.73.stat_ref), custom_call_target="tpu_custom_call" | custom-call | tf_op jit(solution)/shard_map/pallas_call | solution.py:862
  343.2 4.6 all-to-all-start.3
  350.2 28.0 %all-to-all-done.3 = bf16[8,128,640]{2,1,0:T(8,128)(2,1)} async-done(((bf16[8,128,640]{2,1,0:T(8,128)(2,1)}), bf16[8,128,640]{2,1,0:T(8,128)(2,1)}, u32[]{:S(2)}, u32[]{:S(2)}) %all-to-all-start.3) | async-done | bytes 1310752 | tf_op jit(solution)/shard_map/all_to_all | solution.py:1288
  379.7 4.7 multiply_reduce_fusion
  386.6 17.5 %shard_map.347 = (f32[256,768]{1,0:T(8,128)}, f32[1,768]{1,0:T(1,128)}, bf16[768,3072]{1,0:T(8,128)(2,1)}, bf16[3072,768]{1,0:T(8,128)(2,1)}) custom-call(f32[256,768]{1,0:T(8,128)} %add_add_fusion.2.upstream_ref, f32[256,768]{1,0:T(8,128)} %convolution_add_fusion.1.resid_ref, f32[1,768]{1,0:T(1,128)} %get-tuple-element.183.gain_ref, ...), custom_call_target="tpu_custom_call" | custom-call | flops 4831838208 | bytes 37748736 | tf_op jit(solution)/shard_map/pallas_call | solution.py:708
  408.5 21.6 %shard_map.348.later_ref = f32[2,64,768]{2,1,0:T(8,128)} custom-call(f32[2,128,768]{2,1,0:T(8,128)} %get-tuple-element.176.input_ref.grad_ref, f32[64,768]{1,0:T(8,128)} %get-tuple-element.186.decay_ref), custom_call_target="tpu_custom_call" | custom-call | bytes 6291456 | tf_op jit(solution)/shard_map/pallas_call | solution.py:532
  432.3 20.8 %shard_map.349 = (f32[2,128,768]{2,1,0:T(8,128)S(1)}, f32[64,768]{1,0:T(8,128)S(1)}, f32[64,768]{1,0:T(8,128)S(1)}, f32[1,768]{1,0:T(1,128)S(1)}) custom-call(f32[2,128,768]{2,1,0:T(8,128)S(1)} %copy-done.1, f32[2,128,768]{2,1,0:T(8,128)S(1)} %copy-done.2, f32[2,64,768]{2,1,0:T(8,128)S(1)} %copy-done.6, f32[2,64,768]{2,1,0:T(8,128)S(1)} %copy-done.7, ...), custom_call_target="tpu_custom_call" | custom-call | bytes 2755584 | tf_op jit(solution)/shard_map/pallas_call | solution.py:154
  459.0 3.3 convolution_convert_fusion.1
  470.6 98.4 %shard_map.350 = (f32[24,2304]{1,0:T(8,128)}, f32[24,3072]{1,0:T(8,128)}, f32[24,768]{1,0:T(8,128)}, f32[24,2304]{1,0:T(8,128)}, f32[96,768]{1,0:T(8,128)}, /*in...) custom-call(bf16[4,2,2,2,24,2560]{5,4,3,2,1,0:T(8,128)(2,1)} %bitcas, ...), custom_call_target="tpu_custom_call" | custom-call | bytes 78643200 | tf_op jit(solution)/shard_map/pallas_call | solution.py:441
  (268 shorter events, 69.1 us)
Async XLA Ops:
  7.3 150.5 %all-gather.3.cloned.1.call-start = ((), (), s32[]{:S(2)}) async-start(), calls=%async_computation.5 | async-start | bytes 16220160 | tf_op jit(solution)/shard_map/all_gather | solution.py:1213
  8.7 82.9 %copy-start.8 = (bf16[2,128,768]{2,1,0:T(8,128)(2,1)S(1)}, bf16[2,128,768]{2,1,0:T(8,128)(2,1)}, u32[]{:S(2)}) copy-start(bf16[2,128,768]{2,1,0:T(8,128)(2,1)} %param.20) | copy-start | bytes 1179652
  13.1 259.1 %all-gather.5.cloned.1.call-start = ((), (), s32[]{:S(2)}) async-start(), calls=%async_computation.6 | async-start | bytes 4866048 | tf_op jit(solution)/shard_map/all_gather | solution.py:1219
  93.3 291.1 %copy-start.51 = (f32[768]{0:T(1024)}, f32[768]{0:T(1024)S(1)}, u32[]{:S(2)}) copy-start(f32[768]{0:T(1024)S(1)} %get-tuple-element.147) | copy-start | bytes 9220
  96.5 3.4 collective-permute-start
  99.9 29.5 %copy-start.3 = (f32[64,768]{1,0:T(8,128)S(1)}, f32[64,768]{1,0:T(8,128)}, u32[]{:S(2)}) copy-start(f32[64,768]{1,0:T(8,128)} %get-tuple-element.186.decay_ref) | copy-start | bytes 589828
  140.9 29.9 %copy-start.16 = (bf16[2,128,768]{2,1,0:T(8,128)(2,1)}, bf16[2,128,768]{2,1,0:T(8,128)(2,1)S(1)}, u32[]{:S(2)}) copy-start(bf16[2,128,768]{2,1,0:T(8,128)(2,1)S(1)} %convert_element_type.109) | copy-start | bytes 1179652
  172.1 212.3 %copy-start.58 = (f32[256]{0:T(256)}, f32[256]{0:T(256)S(1)}, u32[]{:S(2)}) copy-start(f32[256]{0:T(256)S(1)} %broadcast_multiply_fusion.4) | copy-start | bytes 3076
  173.5 210.9 %copy-start.65 = (f32[256]{0:T(256)}, f32[256]{0:T(256)S(1)}, u32[]{:S(2)}) copy-start(f32[256]{0:T(256)S(1)} %fusion.24) | copy-start | bytes 3076
  177.6 76.7 %copy-start.71 = (s32[2]{0:T(128)S(1)}, s32[2]{0:T(128)}, u32[]{:S(2)}) copy-start(s32[2]{0:T(128)} %param.22) | copy-start | bytes 28
  231.9 22.5 %slice-start = ((bf16[768,10240]{1,0:T(8,128)(2,1)}), bf16[768,768]{1,0:T(8,128)(2,1)S(1)}, s32[]{:S(2)}) async-start(bf16[768,10240]{1,0:T(8,128)(2,1)} %all-gather.3.cloned.1.call-done.up_ref), calls=%async_computation.8 | async-start | bytes 2359296 | tf_op jit(solution)/shard_map/slice | solution.py:1141
  249.9 18.0 %all-to-all-start.1 = ((bf16[8,128,256]{2,1,0:T(8,128)(2,1)}), bf16[8,128,256]{2,1,0:T(8,128)(2,1)}, u32[]{:S(2)}, u32[]{:S(2)}) async-start(bf16[8,128,256]{2,1,0:T(8,128)(2,1)} %bitcast.136), calls=%async_computation.1 | async-start | bytes 1048576 | tf_op jit(solution)/shard_map/all_to_all | solution.py:1288
  254.1 318.1 %reduce-scatter.2.cloned.1.call-start = ((), (), s32[]{:S(2)}) async-start(), calls=%async_computation.7 | async-start | bytes 9732096 | tf_op jit(solution)/shard_map/reduce_scatter | solution.py:1339
  269.1 13.6 %copy-start.38 = (bf16[2,1,128,256]{3,2,1,0:T(8,128)(2,1)}, bf16[2,1,128,256]{3,2,1,0:T(8,128)(2,1)S(1)}, u32[]{:S(2)}) copy-start(bf16[2,1,128,256]{3,2,1,0:T(8,128)(2,1)S(1)} %get-tuple-element.193) | copy-start | bytes 393220
  269.1 13.5 %copy-start.40 = (bf16[2,1,128,256]{3,2,1,0:T(8,128)(2,1)}, bf16[2,1,128,256]{3,2,1,0:T(8,128)(2,1)S(1)}, u32[]{:S(2)}) copy-start(bf16[2,1,128,256]{3,2,1,0:T(8,128)(2,1)S(1)} %get-tuple-element.194) | copy-start | bytes 393220
  343.2 35.0 %all-to-all-start.3 = ((bf16[8,128,640]{2,1,0:T(8,128)(2,1)}), bf16[8,128,640]{2,1,0:T(8,128)(2,1)}, u32[]{:S(2)}, u32[]{:S(2)}) async-start(bf16[8,128,640]{2,1,0:T(8,128)(2,1)} %bitcast.37), calls=%async_computation.3 | async-start | bytes 2621440 | tf_op jit(solution)/shard_map/all_to_all | solution.py:1288
  349.1 30.6 %copy-start.11 = (f32[256,768]{1,0:T(8,128)S(1)}, f32[256,768]{1,0:T(8,128)}, u32[]{:S(2)}) copy-start(f32[256,768]{1,0:T(8,128)} %get-tuple-element.64) | copy-start | bytes 2359300
  406.1 24.1 %copy-start.1 = (f32[2,128,768]{2,1,0:T(8,128)S(1)}, f32[2,128,768]{2,1,0:T(8,128)}, u32[]{:S(2)}) copy-start(f32[2,128,768]{2,1,0:T(8,128)} %get-tuple-element.161.input_ref) | copy-start | bytes 2359300
  406.1 24.1 %copy-start.4 = (f32[64,768]{1,0:T(8,128)S(1)}, f32[64,768]{1,0:T(8,128)}, u32[]{:S(2)}) copy-start(f32[64,768]{1,0:T(8,128)} %get-tuple-element.186.decay_ref) | copy-start | bytes 589828
  406.1 24.1 %copy-start.6 = (f32[2,64,768]{2,1,0:T(8,128)S(1)}, f32[2,64,768]{2,1,0:T(8,128)}, u32[]{:S(2)}) copy-start(f32[2,64,768]{2,1,0:T(8,128)} %shard_map.340.carried_ref) | copy-start | bytes 1179652
  432.3 20.8 %copy-start.10 = (f32[2,128,2304]{2,1,0:T(8,128)S(1)}, f32[2,128,2304]{2,1,0:T(8,128)}, u32[]{:S(2)}) copy-start(f32[2,128,2304]{2,1,0:T(8,128)} %copy-done.9) | copy-start | bytes 7077892
  455.2 7.2 %collective-permute-start.1 = (f32[2,3,768]{2,1,0:T(4,128)S(1)}, f32[2,3,768]{2,1,0:T(4,128)S(1)}, u32[]{:S(2)}, u32[]{:S(2)}) collective-permute-start(f32[2,3,768]{2,1,0:T(4,128)S(1)} %pad_add_fusion.1), channel_id=1, source_target_pairs={{4,0},{8,4},{12,8},{16,12},{20,16},{24,20},{28,24},{5,1},{9,5},{13... | collective-permute-start | bytes 55304 | tf_op jit(solution)/shard_map/ppermute | solution.py:183
  569.0 11.3 %copy-start.37 = (f32[24,2304]{1,0:T(8,128)S(1)}, f32[24,2304]{1,0:T(8,128)}, u32[]{:S(2)}) copy-start(f32[24,2304]{1,0:T(8,128)} %get-tuple-element.241) | copy-start | bytes 663556
  569.0 12.0 %copy-start.44 = (f32[24,768]{1,0:T(8,128)S(1)}, f32[24,768]{1,0:T(8,128)}, u32[]{:S(2)}) copy-start(f32[24,768]{1,0:T(8,128)} %get-tuple-element.242) | copy-start | bytes 221188
  (61 other events, 252.5 us)
Sparse Core Ops, SparseCore 0:
  13.2 144.5 all-gather.2
  160.7 72.4 all-gather.4
  343.3 143.1 reduce-scatter.1

commit v2 on v0

--- a/solution.py
+++ b/solution.py
@@ -362,11 +362,10 @@
             started[chunk, 0].wait_recv()
             loads[chunk].wait()
 
-            @pl.loop(0, box[0])
-            def _(row):
-                for i in range(2):
-                    for j in range(2):
-                        held[row, i, j] = add_into(held[row, i, j], from_core[row, i, j])
+            @pl.loop(0, 4 * box[0])
+            def _(turn):
+                at = (lax.div(turn, 4), lax.rem(lax.div(turn, 2), 2), lax.rem(turn, 2))
+                held[at] = add_into(held[at], from_core[at])
 
             if x_first:
                 push(chunk, 1, held.at[:, :, 1 - y], from_one, to_y)
@@ -375,13 +374,11 @@
         elif stage == 1:
             started[chunk, 1].wait_recv()
 
-            @pl.loop(0, box[0])
-            def _(row):
-                for i in range(2):
-                    if x_first:
-                        held[row, i, y] = add_into(held[row, i, y], from_one[row, i])
-                    else:
-                        held[row, x, i] = add_into(held[row, x, i], from_one[row, i])
+            @pl.loop(0, 2 * box[0])
+            def _(turn):
+                row, i = lax.div(turn, 2), lax.rem(turn, 2)
+                at = (row, i, y) if x_first else (row, x, i)
+                held[at] = add_into(held[at], from_one[row, i])
 
             if not line_last:
                 for step in range(1, box[0]):
@@ -482,13 +479,15 @@
         peer = (lax.rem(me + step, count), batch)
         pl.semaphore_signal(barrier, inc=1, device_id=peer, device_id_type=MESH)
 
-    for tile in range(width // lanes):
-        columns = slice(tile * lanes, (tile + 1) * lanes)
+    @pl.loop(0, width // lanes)
+    def _(tile):
+        columns = pl.ds(pl.multiple_of(tile * lanes, lanes), lanes)
         encode_kernel(reverse, input_ref.at[:, :, columns], decay_ref.at[:, columns], ends)
         for group in range(count):
             rows = slice(group * part, (group + 1) * part)
             mine = jnp.concatenate([ends[seq, rows] for seq in range(seq_count)], axis=0)
             outgoing[group, :, columns] = mine.astype(bf16)
+
     pl.semaphore_wait(barrier, count - 1)
 
     def exchange(phase, source, target):
@@ -556,7 +555,7 @@
         out_ref[...] = resid
 
     hidden = jnp.dot(normed_ref[...], up_ref[...], preferred_element_type=f32)
-    hidden_ref[...] = hidden
+    hidden_ref[...] = hidden.astype(bf16)
     bend = jnp.tanh(gelu_scale * (hidden + gelu_cubic * hidden * hidden * hidden))
     active = (0.5 * hidden * (1.0 + bend)).astype(bf16)
     active_ref[...] = active
@@ -582,7 +581,7 @@
         out_shape=[
             shaped(rows, width),
             shaped(rows, width, dtype=bf16),
-            shaped(rows, inner),
+            shaped(rows, inner, dtype=bf16),
             shaped(rows, inner, dtype=bf16),
         ],
         cost_estimate=pl.CostEstimate(
@@ -613,7 +612,7 @@
     along = (((0,), (0,)), ((), ()))
     upstream_low = upstream_ref[...].astype(bf16)
     into_active = lax.dot_general(upstream_low, down_ref[...], across, preferred_element_type=f32)
-    hidden = hidden_ref[...]
+    hidden = hidden_ref[...].astype(f32)
     square = hidden * hidden
     bend = jnp.tanh(gelu_scale * hidden * (1.0 + gelu_cubic * square))
     slope = 0.5 * (1.0 + bend) + 0.5 * hidden * (1.0 - bend * bend) * (
@@ -1375,7 +1374,7 @@
     if by_kernel:
         last += [first_down_grad, attend_output_grad]
         orders = ("yxz", "xyz", "xzy", "yxz", "xyz", "yzx")
-        plan = chunked([g.shape[1] for g in last], (6, 6, 2, 6, 2, 4, 2), orders)
+        plan = chunked([g.shape[1] for g in last], (4, 4, 2, 4, 2, 4, 2), orders)
         part = attend_cols // 3 // groups
 
         def finish(index, block, results):

time: 567 us -> 563 us (level)
  no operation moved by 1% of the time
where the time goes in v2:
time: 563 us; the launch traced here: 553 us
  Pallas kernels  321 us (57%)
  blocking collectives  67.2 us (12%)
  waiting for transfers between devices  56.5 us (10%)
  local copies, waits for them, and re-layouts  38.4 us (7%)
  matrix products  26.8 us (5%)
  between operations  15.6 us (3%)
  other arithmetic  15.1 us (3%)
  starting transfers between devices  12.6 us (2%)
    pallas_call x1, Pallas kernels, scatter_blocks(): pl.pallas_call(functools.partial(scatter_kernel, plan, gap, finish, (len(...  103 us
    pallas_call x1, Pallas kernels, gather_blocks(): pl.pallas_call(functools.partial(gather_kernel, plan, gap), out_shape=out...  75.8 us
    all_to_all x2, blocking collectives, deal(): lax.all_to_all(parts, 'seq', split_axis=0, concat_axis=0, tiled=True)  67.2 us
    pallas_call x2, Pallas kernels, carried_by_kernel(): pl.pallas_call(functools.partial(carry_kernel, reverse), out_shape=shaped...  51.4 us
    all_to_all x2, waiting for transfers between devices, collect(): back = lax.all_to_all(parts, 'seq', split_axis=0, concat_axis=0, tiled=True)  40.2 us
    pallas_call x2, Pallas kernels, per_lane_tile(): pl.pallas_call(kernel, grid=(args[0].shape[-1] // lanes,), in_specs=[spec...  30.1 us
    unnamed x169, local copies, waits for them, and re-layouts  26.1 us
    pallas_call x2, Pallas kernels, feed_back_blocks(): pl.pallas_call(functools.partial(feed_back_kernel, packed), grid=(inner /...  25.1 us
  transfers between devices with their start and end apart: 7, of which 4 were waited for; matrix products, arithmetic and copies ran while one was open for 9% of the time, Pallas kernels for 52%

profile of v2, /device:TPU:0, one launch (start us, length us, event | category | flops | bytes accessed | tf_op | source)
XLA Modules:
  0.0 553.0 jit_solution(14224288280775454401)
XLA Ops:
  14.6 75.8 %shard_map.339 = (bf16[4,2,2,2,24,2560]{5,4,3,2,1,0:T(8,128)(2,1)}, bf16[4,2,2,2,96,768]{5,4,3,2,1,0:T(8,128)(2,1)}) custom-call(bf16[24,2560]{1,0:T(8,128)(2,1)} %fusion.22.refs_0_, bf16[96,768]{1,0:T(8,128)(2,1)} %refs_1_.1), custom_call_target="tpu_custom_call" | custom-call | bytes 17301504 | tf_op jit(solution)/shard_map/pallas_call | solution.py:305
  92.1 3.4 fusion
  100.5 29.4 %shard_map.340.carried_ref = f32[2,64,768]{2,1,0:T(8,128)} custom-call(f32[2,128,768]{2,1,0:T(8,128)} %get-tuple-element.161.input_ref, f32[64,768]{1,0:T(8,128)} %get-tuple-element.186.decay_ref), custom_call_target="tpu_custom_call" | custom-call | bytes 6291456 | tf_op jit(solution)/shard_map/pallas_call | solution.py:532
  132.1 9.3 %shard_map.341 = (f32[2,128,768]{2,1,0:T(8,128)S(1)}, f32[2,128,768]{2,1,0:T(8,128)S(1)}) custom-call(f32[2,128,768]{2,1,0:T(8,128)S(1)} %copy-done.2, f32[2,128,768]{2,1,0:T(8,128)S(1)} %get-tuple-element.163.query_ref, f32[2,64,768]{2,1,0:T(8,128)S(1)} %copy-done.7, f32[64,768]{1,0:T(8,128)S(1)} %copy-done.5, f32[64,768]{1,0:T(8,128)S(1)} %get-tuple-element.185.weight_ref, ...), custom_call_target="tpu_custom_call" | custom-call | bytes 2362368 | tf_op jit(solution)/shard_map/pallas_call | solution.py:154
  142.3 15.6 %all-gather.3.cloned.1.call-done.up_ref = bf16[768,10240]{1,0:T(8,128)(2,1)} async-done(((bf16[24,10240]{1,0:T(8,128)(2,1)}), bf16[768,10240]{1,0:T(8,128)(2,1)}) %all-gather.3.cloned.1.call-update) | async-done | bytes 15728656 | tf_op jit(solution)/shard_map/all_gather | solution.py:1187
  162.0 5.9 %shard_map.342 = (f32[256,768]{1,0:T(8,128)S(1)}, bf16[256,768]{1,0:T(8,128)(2,1)S(1)}, bf16[256,3072]{1,0:T(8,128)(2,1)S(1)}, bf16[256,3072]{1,0:T(8,128)(2,1)S(1)}) custom-call(f32[256,768]{1,0:T(8,128)S(1)} %convolution_add_fusion.1.resid_ref, f32[1,768]{1,0:T(1,128)S(1)} %get-tuple-element.183.gain_ref, ...), custom_call_target="tpu_custom_call" | custom-call | flops 2415919104 | bytes 23592960 | tf_op jit(solution)/shard_map/pallas_call | solution.py:571
  170.2 3.5 convolution_convert_fusion.2
  174.2 49.9 %all_to_all.20 = bf16[8,128,640]{2,1,0:T(8,128)(2,1)} all-to-all(bf16[8,128,640]{2,1,0:T(8,128)(2,1)S(1)} %bitcast.118), channel_id=1, replica_groups=mesh['seq'=8,'batch'=4] {'seq'}, dimensions={0} | all-to-all | bytes 2621440 | tf_op jit(solution)/shard_map/all_to_all | solution.py:1257
  224.1 11.1 %shard_map.343 = (bf16[1024,256]{1,0:T(8,128)(2,1)}, f32[1024,192]{1,0:T(8,128)}, f32[3,1024,128]{2,1,0:T(8,128)}) custom-call(bf16[1024,640]{1,0:T(8,128)(2,1)} %bitcast.113), custom_call_target="tpu_custom_call" | custom-call | tf_op jit(solution)/shard_map/pallas_call | solution.py:819
  235.2 4.1 all-to-all-start.1
  241.0 11.4 %all-to-all-done.1 = bf16[8,128,256]{2,1,0:T(8,128)(2,1)} async-done(((bf16[8,128,256]{2,1,0:T(8,128)(2,1)}), bf16[8,128,256]{2,1,0:T(8,128)(2,1)}, u32[]{:S(2)}, u32[]{:S(2)}) %all-to-all-start.1) | async-done | bytes 524320 | tf_op jit(solution)/shard_map/all_to_all | solution.py:1262
  258.0 6.0 %shard_map.344 = (f32[256,768]{1,0:T(8,128)S(1)}, bf16[256,768]{1,0:T(8,128)(2,1)S(1)}, bf16[256,3072]{1,0:T(8,128)(2,1)S(1)}, bf16[256,3072]{1,0:T(8,128)(2,1)S(1)}) custom-call(f32[256,768]{1,0:T(8,128)S(1)} %convolution_add_fusion.resid_ref, f32[1,768]{1,0:T(1,128)S(1)} %get-tuple-element.182.gain_ref, ...), custom_call_target="tpu_custom_call" | custom-call | flops 2415919104 | bytes 23592960 | tf_op jit(solution)/shard_map/pallas_call | solution.py:571
  264.9 12.9 %shard_map.345 = (f32[256,768]{1,0:T(8,128)S(1)}, f32[1,768]{1,0:T(1,128)S(1)}, bf16[768,6144]{1,0:T(8,128)(2,1)}) custom-call(f32[256,768]{1,0:T(8,128)S(1)} %bitcast.110, f32[256,768]{1,0:T(8,128)S(1)} %convolution_add_fusion.resid_ref, f32[1,768]{1,0:T(1,128)S(1)} %get-tuple-element.182.gain_ref, bf16[256,768]{1,0:T(8,128)(2,1)S(1)} %get-tuple-element.68.normed_ref, ...), custom_call_target="tpu_custom_call" | custom-call | flops 4831838208 | bytes 37748736 | tf_op jit(solution)/shard_map/pallas_call | solution.py:708
  278.6 17.3 %all_to_all.21 = bf16[8,128,256]{2,1,0:T(8,128)(2,1)} all-to-all(bf16[8,128,256]{2,1,0:T(8,128)(2,1)S(1)} %bitcast.129), channel_id=1, replica_groups=mesh['seq'=8,'batch'=4] {'seq'}, dimensions={0} | all-to-all | bytes 1048576 | tf_op jit(solution)/shard_map/all_to_all | solution.py:1257
  295.9 12.4 %shard_map.346 = bf16[1024,640]{1,0:T(8,128)(2,1)} custom-call(bf16[1024,640]{1,0:T(8,128)(2,1)} %bitcast.114, bf16[1024,256]{1,0:T(8,128)(2,1)} %bitcast.131, f32[1024,192]{1,0:T(8,128)} %get-tuple-element.72.full_ref, f32[3,1024,128]{2,1,0:T(8,128)} %get-tuple-element.73.stat_ref), custom_call_target="tpu_custom_call" | custom-call | tf_op jit(solution)/shard_map/pallas_call | solution.py:836
  308.4 4.6 all-to-all-start.3
  314.8 28.8 %all-to-all-done.3 = bf16[8,128,640]{2,1,0:T(8,128)(2,1)} async-done(((bf16[8,128,640]{2,1,0:T(8,128)(2,1)}), bf16[8,128,640]{2,1,0:T(8,128)(2,1)}, u32[]{:S(2)}, u32[]{:S(2)}) %all-to-all-start.3) | async-done | bytes 1310752 | tf_op jit(solution)/shard_map/all_to_all | solution.py:1262
  345.2 4.1 multiply_reduce_fusion
  351.3 12.3 %shard_map.347 = (f32[256,768]{1,0:T(8,128)S(1)}, f32[1,768]{1,0:T(1,128)S(1)}, bf16[768,3072]{1,0:T(8,128)(2,1)}, bf16[3072,768]{1,0:T(8,128)(2,1)}) custom-call(f32[256,768]{1,0:T(8,128)S(1)} %add_add_fusion.2.upstream_ref, f32[256,768]{1,0:T(8,128)S(1)} %convolution_add_fusion.1.resid_ref, f32[1,768]{1,0:T(1,128)S(1)} %get-tuple-element.183.gain_ref, ...), custom_call_target="tpu_custom_call" | custom-call | flops 4831838208 | bytes 37748736 | tf_op jit(solution)/shard_map/pallas_call | solution.py:708
  367.8 22.0 %shard_map.348.later_ref = f32[2,64,768]{2,1,0:T(8,128)} custom-call(f32[2,128,768]{2,1,0:T(8,128)} %get-tuple-element.176.input_ref.grad_ref, f32[64,768]{1,0:T(8,128)} %get-tuple-element.186.decay_ref), custom_call_target="tpu_custom_call" | custom-call | bytes 6291456 | tf_op jit(solution)/shard_map/pallas_call | solution.py:532
  392.0 20.8 %shard_map.349 = (f32[2,128,768]{2,1,0:T(8,128)S(1)}, f32[64,768]{1,0:T(8,128)S(1)}, f32[64,768]{1,0:T(8,128)S(1)}, f32[1,768]{1,0:T(1,128)S(1)}) custom-call(f32[2,128,768]{2,1,0:T(8,128)S(1)} %copy-done.3, f32[2,128,768]{2,1,0:T(8,128)S(1)} %copy-done.4, f32[2,64,768]{2,1,0:T(8,128)S(1)} %copy-done.8, f32[2,64,768]{2,1,0:T(8,128)S(1)} %copy-done.9, ...), custom_call_target="tpu_custom_call" | custom-call | bytes 2755584 | tf_op jit(solution)/shard_map/pallas_call | solution.py:154
  420.1 3.3 convolution_convert_fusion.1
  427.6 2.9 convolution_convert_fusion
  430.4 102.9 %shard_map.350 = (f32[24,2304]{1,0:T(8,128)}, f32[24,3072]{1,0:T(8,128)}, f32[24,768]{1,0:T(8,128)}, f32[24,2304]{1,0:T(8,128)}, f32[96,768]{1,0:T(8,128)}, /*in...) custom-call(bf16[4,2,2,2,24,2560]{5,4,3,2,1,0:T(8,128)(2,1)} %bitcas, ...), custom_call_target="tpu_custom_call" | custom-call | bytes 78643200 | tf_op jit(solution)/shard_map/pallas_call | solution.py:441
  (266 shorter events, 67.7 us)
Async XLA Ops:
  7.3 150.6 %all-gather.3.cloned.1.call-start = ((), (), s32[]{:S(2)}) async-start(), calls=%async_computation.5 | async-start | bytes 16220160 | tf_op jit(solution)/shard_map/all_gather | solution.py:1187
  8.7 82.9 %copy-start.18 = (bf16[2,128,768]{2,1,0:T(8,128)(2,1)S(1)}, bf16[2,128,768]{2,1,0:T(8,128)(2,1)}, u32[]{:S(2)}) copy-start(bf16[2,128,768]{2,1,0:T(8,128)(2,1)} %param.20) | copy-start | bytes 1179652
  13.1 242.6 %all-gather.5.cloned.1.call-start = ((), (), s32[]{:S(2)}) async-start(), calls=%async_computation.6 | async-start | bytes 4866048 | tf_op jit(solution)/shard_map/all_gather | solution.py:1193
  95.6 3.4 collective-permute-start
  98.9 30.9 %copy-start.5 = (f32[64,768]{1,0:T(8,128)S(1)}, f32[64,768]{1,0:T(8,128)}, u32[]{:S(2)}) copy-start(f32[64,768]{1,0:T(8,128)} %get-tuple-element.186.decay_ref) | copy-start | bytes 589828
  142.3 17.4 %copy-start.26 = (bf16[2,128,768]{2,1,0:T(8,128)(2,1)}, bf16[2,128,768]{2,1,0:T(8,128)(2,1)S(1)}, u32[]{:S(2)}) copy-start(bf16[2,128,768]{2,1,0:T(8,128)(2,1)S(1)} %convert_element_type.109) | copy-start | bytes 1179652
  174.2 65.4 %copy-start.70 = (s32[2]{0:T(128)S(1)}, s32[2]{0:T(128)}, u32[]{:S(2)}) copy-start(s32[2]{0:T(128)} %param.22) | copy-start | bytes 28
  224.1 15.6 %slice-start = ((bf16[768,10240]{1,0:T(8,128)(2,1)}), bf16[768,768]{1,0:T(8,128)(2,1)S(1)}, s32[]{:S(2)}) async-start(bf16[768,10240]{1,0:T(8,128)(2,1)} %all-gather.3.cloned.1.call-done.up_ref), calls=%async_computation.8 | async-start | bytes 2359296 | tf_op jit(solution)/shard_map/slice | solution.py:1115
  235.2 17.1 %all-to-all-start.1 = ((bf16[8,128,256]{2,1,0:T(8,128)(2,1)}), bf16[8,128,256]{2,1,0:T(8,128)(2,1)}, u32[]{:S(2)}, u32[]{:S(2)}) async-start(bf16[8,128,256]{2,1,0:T(8,128)(2,1)} %bitcast.137), calls=%async_computation.1 | async-start | bytes 1048576 | tf_op jit(solution)/shard_map/all_to_all | solution.py:1262
  239.4 297.2 %reduce-scatter.2.cloned.1.call-start = ((), (), s32[]{:S(2)}) async-start(), calls=%async_computation.7 | async-start | bytes 9732096 | tf_op jit(solution)/shard_map/reduce_scatter | solution.py:1313
  264.9 12.9 %copy-start.23 = (bf16[4,256,768]{2,1,0:T(8,128)(2,1)S(1)}, bf16[4,256,768]{2,1,0:T(8,128)(2,1)}, u32[]{:S(2)}) copy-start(bf16[4,256,768]{2,1,0:T(8,128)(2,1)} %pad.47) | copy-start | bytes 4718596
  308.4 35.2 %all-to-all-start.3 = ((bf16[8,128,640]{2,1,0:T(8,128)(2,1)}), bf16[8,128,640]{2,1,0:T(8,128)(2,1)}, u32[]{:S(2)}, u32[]{:S(2)}) async-start(bf16[8,128,640]{2,1,0:T(8,128)(2,1)} %bitcast.119), calls=%async_computation.3 | async-start | bytes 2621440 | tf_op jit(solution)/shard_map/all_to_all | solution.py:1262
  313.7 31.4 %copy-start.68 = (f32[256]{0:T(256)S(1)}, f32[256]{0:T(256)}, u32[]{:S(2)}) copy-start(f32[256]{0:T(256)} %copy-done.67) | copy-start | bytes 3076
  365.4 24.5 %copy-start.3 = (f32[2,128,768]{2,1,0:T(8,128)S(1)}, f32[2,128,768]{2,1,0:T(8,128)}, u32[]{:S(2)}) copy-start(f32[2,128,768]{2,1,0:T(8,128)} %get-tuple-element.161.input_ref) | copy-start | bytes 2359300
  365.4 24.5 %copy-start.6 = (f32[64,768]{1,0:T(8,128)S(1)}, f32[64,768]{1,0:T(8,128)}, u32[]{:S(2)}) copy-start(f32[64,768]{1,0:T(8,128)} %get-tuple-element.186.decay_ref) | copy-start | bytes 589828
  365.4 24.5 %copy-start.8 = (f32[2,64,768]{2,1,0:T(8,128)S(1)}, f32[2,64,768]{2,1,0:T(8,128)}, u32[]{:S(2)}) copy-start(f32[2,64,768]{2,1,0:T(8,128)} %shard_map.340.carried_ref) | copy-start | bytes 1179652
  392.0 20.8 %copy-start.21 = (f32[2,128,2304]{2,1,0:T(8,128)S(1)}, f32[2,128,2304]{2,1,0:T(8,128)}, u32[]{:S(2)}) copy-start(f32[2,128,2304]{2,1,0:T(8,128)} %copy-done.20) | copy-start | bytes 7077892
  415.8 7.6 %collective-permute-start.1 = (f32[2,3,768]{2,1,0:T(4,128)S(1)}, f32[2,3,768]{2,1,0:T(4,128)S(1)}, u32[]{:S(2)}, u32[]{:S(2)}) collective-permute-start(f32[2,3,768]{2,1,0:T(4,128)S(1)} %pad_add_fusion.1), channel_id=1, source_target_pairs={{4,0},{8,4},{12,8},{16,12},{20,16},{24,20},{28,24},{5,1},{9,5},{13... | collective-permute-start | bytes 55304 | tf_op jit(solution)/shard_map/ppermute | solution.py:183
  533.4 8.7 %copy-start.59 = (f32[24,64]{1,0:T(8,128)S(1)}, f32[24,64]{1,0:T(8,128)}, u32[]{:S(2)}) copy-start(f32[24,64]{1,0:T(8,128)} %get-tuple-element.234) | copy-start | bytes 18436
  533.4 9.3 %copy-start.57 = (f32[24,768]{1,0:T(8,128)S(1)}, f32[24,768]{1,0:T(8,128)}, u32[]{:S(2)}) copy-start(f32[24,768]{1,0:T(8,128)} %get-tuple-element.236) | copy-start | bytes 221188
  533.4 9.9 %copy-start.47 = (f32[24,3072]{1,0:T(8,128)S(1)}, f32[24,3072]{1,0:T(8,128)}, u32[]{:S(2)}) copy-start(f32[24,3072]{1,0:T(8,128)} %get-tuple-element.238) | copy-start | bytes 884740
  533.4 10.6 %copy-start.46 = (f32[96,768]{1,0:T(8,128)S(1)}, f32[96,768]{1,0:T(8,128)}, u32[]{:S(2)}) copy-start(f32[96,768]{1,0:T(8,128)} %get-tuple-element.239) | copy-start | bytes 884740
  533.4 11.3 %copy-start.48 = (f32[24,2304]{1,0:T(8,128)S(1)}, f32[24,2304]{1,0:T(8,128)}, u32[]{:S(2)}) copy-start(f32[24,2304]{1,0:T(8,128)} %get-tuple-element.241) | copy-start | bytes 663556
  533.4 12.0 %copy-start.56 = (f32[24,768]{1,0:T(8,128)S(1)}, f32[24,768]{1,0:T(8,128)}, u32[]{:S(2)}) copy-start(f32[24,768]{1,0:T(8,128)} %get-tuple-element.242) | copy-start | bytes 221188
  (60 other events, 208.8 us)
Sparse Core Ops, SparseCore 0:
  13.2 144.6 all-gather.2
  160.8 69.0 all-gather.4
  308.5 146.4 reduce-scatter.1

commit v3 on v2

--- a/solution.py
+++ b/solution.py
@@ -221,11 +221,13 @@
     return lax.rem(z + step, box[0])
 
 
-def greet():
+def greet(diagonal=False):
     z, x, y, core = here()
     barrier = pltpu.get_barrier_semaphore()
     peers = [device(line_peer(z, step), x, y, core) for step in range(1, box[0])]
     peers += [device(z, 1 - x, y, core), device(z, x, 1 - y, core), device(z, x, y, 1 - core)]
+    if diagonal:
+        peers += [device(line_peer(z, step), 1 - x, y, core) for step in range(1, box[0])]
     for peer in peers:
         pl.semaphore_signal(barrier, inc=1, device_id=peer, device_id_type=MESH)
     pl.semaphore_wait(barrier, len(peers))
@@ -322,13 +324,17 @@
     return (total.astype(f32) + other.astype(f32)).astype(bf16)
 
 
-def scatter_kernel(plan, gap, finish, counts, *refs):
-    count, out_count = counts
-    ins, results = refs[:count], refs[count : count + out_count]
-    outs, buffers = refs[count + out_count : 2 * count + out_count], refs[2 * count + out_count : -3]
-    send, receive, local = refs[-3:]
+def scatter_kernel(plan, gap, finish, beside, counts, *refs):
+    count, out_count, work_ins, work_outs, work_scratch = counts
+    refs, taken = list(refs), []
+    for number in (count, work_ins, out_count, work_outs, count, work_scratch):
+        taken.append(refs[:number])
+        refs = refs[number:]
+    ins, work_in_refs, results, work_out_refs, outs, work_refs = taken
+    buffers, (send, receive, local) = refs[:-3], refs[-3:]
     z, x, y, core = here()
-    greet()
+    greet(diagonal=beside is not None)
+    work = list(beside(*work_in_refs, *work_out_refs, *work_refs)) if beside else []
     started = {}
 
     def push(chunk, slot, source, target, peer):
@@ -353,7 +359,10 @@
         load.start()
         loads.append(load)
 
-    for stage, chunk in staggered(len(plan), 4, gap):
+    steps, pieces = list(staggered(len(plan), 4, gap)), len(work)
+    for turn, (stage, chunk) in enumerate(steps):
+        while work and turn * pieces >= (pieces - len(work)) * len(steps) * 3 // 4:
+            work.pop(0)()
         index, first, width, order = plan[chunk]
         x_first, line_last = order[0] == "y", order[-1] == "z"
         held, from_core, from_one, from_two, from_line = buffers[5 * chunk : 5 * chunk + 5]
@@ -429,20 +438,23 @@
             started[chunk, slot].wait_send()
 
 
-def scatter_blocks(grads, plan, finish, results, gap=2, collective=1):
+def scatter_blocks(grads, plan, finish, results, gap=2, collective=1, work=None):
     views = [g.reshape(box + (g.shape[0] // 32, g.shape[1])) for g in grads]
-    scratch = [pltpu.VMEM(v.shape[4:], f32) for v in views]
+    beside, work_ins, work_outs, work_scratch = work or (None, [], [], [])
+    scratch = [pltpu.VMEM(v.shape[4:], f32) for v in views] + list(work_scratch)
     for index, _, width, order in plan:
         tile = (views[index].shape[4], width)
         ends_of = ((4,), (3,)) if order[-1] == "z" else ((), (3, 2))
         for lead in ((4, 2, 2), (4, 2, 2), (4, 2)) + ends_of:
             scratch.append(pltpu.VMEM(lead + tile, bf16))
+    counts = (len(views), len(results), len(work_ins), len(work_outs), len(work_scratch))
     sent = sum(v.size * v.dtype.itemsize for v in views)
+    local = pl.BlockSpec(memory_space=pltpu.VMEM)
     return pl.pallas_call(
-        functools.partial(scatter_kernel, plan, gap, finish, (len(views), len(results))),
-        out_shape=list(results),
-        in_specs=[pl.BlockSpec(memory_space=pl.ANY)] * len(views),
-        out_specs=[pl.BlockSpec(memory_space=pltpu.VMEM)] * len(results),
+        functools.partial(scatter_kernel, plan, gap, finish, beside, counts),
+        out_shape=list(results) + list(work_outs),
+        in_specs=[pl.BlockSpec(memory_space=pl.ANY)] * len(views) + [local] * len(work_ins),
+        out_specs=[local] * (len(results) + len(work_outs)),
         scratch_shapes=scratch
         + [
             pltpu.SemaphoreType.DMA((len(plan), 6)),
@@ -453,7 +465,7 @@
         compiler_params=pltpu.CompilerParams(
             collective_id=collective, has_side_effects=True, vmem_limit_bytes=60 * 1024 * 1024
         ),
-    )(*views)
+    )(*views, *work_ins)
 
 
 def chunked(widths, pieces, orders):
@@ -466,33 +478,27 @@
     return plan
 
 
-def carry_kernel(
+def carry_pieces(
     reverse, input_ref, decay_ref, carried_ref, ends, outgoing, arrived, joined, final, send, receive
 ):
     seq_count, step_count, width = input_ref.shape
     count = lax.axis_size("seq")
     part = decay_ref.shape[0] // count
     me, batch = lax.axis_index("seq"), lax.axis_index("batch")
-    others = range(1, count)
-    barrier = pltpu.get_barrier_semaphore()
-    for step in others:
-        peer = (lax.rem(me + step, count), batch)
-        pl.semaphore_signal(barrier, inc=1, device_id=peer, device_id_type=MESH)
-
-    @pl.loop(0, width // lanes)
-    def _(tile):
-        columns = pl.ds(pl.multiple_of(tile * lanes, lanes), lanes)
-        encode_kernel(reverse, input_ref.at[:, :, columns], decay_ref.at[:, columns], ends)
-        for group in range(count):
-            rows = slice(group * part, (group + 1) * part)
-            mine = jnp.concatenate([ends[seq, rows] for seq in range(seq_count)], axis=0)
-            outgoing[group, :, columns] = mine.astype(bf16)
-
-    pl.semaphore_wait(barrier, count - 1)
-
-    def exchange(phase, source, target):
+
+    def encode_all():
+        @pl.loop(0, width // lanes)
+        def _(tile):
+            columns = pl.ds(pl.multiple_of(tile * lanes, lanes), lanes)
+            encode_kernel(reverse, input_ref.at[:, :, columns], decay_ref.at[:, columns], ends)
+            for group in range(count):
+                rows = slice(group * part, (group + 1) * part)
+                mine = jnp.concatenate([ends[seq, rows] for seq in range(seq_count)], axis=0)
+                outgoing[group, :, columns] = mine.astype(bf16)
+
+    def started(phase, source, target):
         copies = []
-        for step in others:
+        for step in range(1, count):
             peer = lax.rem(me + step, count)
             copy = pltpu.make_async_remote_copy(
                 src_ref=source.at[peer],
@@ -505,23 +511,88 @@
             copy.start()
             copies.append(copy)
         target[me] = source[me]
-        for copy in copies:
+        return copies
+
+    flying = []
+
+    def first():
+        encode_all()
+        flying.append(started(0, outgoing, arrived))
+
+    def second():
+        for copy in flying.pop():
             copy.wait()
-
-    exchange(0, outgoing, arrived)
-    rates = decay_ref[pl.ds(pl.multiple_of(me * part, part), part), :]
-    power = jnp.exp(-rates * step_count)
-    power = jnp.concatenate([power] * seq_count, axis=0)
-    state = jnp.zeros(power.shape, f32)
-    for block in reversed(range(count)) if reverse else range(count):
-        joined[block] = state.astype(bf16)
-        state = power * state + arrived[block].astype(f32)
-    exchange(1, joined, final)
-    for group in range(count):
-        rows = slice(group * part, (group + 1) * part)
-        found = final[group].astype(f32)
-        for seq in range(seq_count):
-            carried_ref[seq, rows] = found[seq * part : (seq + 1) * part]
+        rates = decay_ref[pl.ds(pl.multiple_of(me * part, part), part), :]
+        power = jnp.exp(-rates * step_count)
+        power = jnp.concatenate([power] * seq_count, axis=0)
+        state = jnp.zeros(power.shape, f32)
+        for block in reversed(range(count)) if reverse else range(count):
+            joined[block] = state.astype(bf16)
+            state = power * state + arrived[block].astype(f32)
+        flying.append(started(1, joined, final))
+
+    def third():
+        for copy in flying.pop():
+            copy.wait()
+        for group in range(count):
+            rows = slice(group * part, (group + 1) * part)
+            found = final[group].astype(f32)
+            for seq in range(seq_count):
+                carried_ref[seq, rows] = found[seq * part : (seq + 1) * part]
+
+    return first, second, third
+
+
+def carry_kernel(reverse, *refs):
+    count = lax.axis_size("seq")
+    me, batch = lax.axis_index("seq"), lax.axis_index("batch")
+    barrier = pltpu.get_barrier_semaphore()
+    for step in range(1, count):
+        peer = (lax.rem(me + step, count), batch)
+        pl.semaphore_signal(barrier, inc=1, device_id=peer, device_id_type=MESH)
+    pl.semaphore_wait(barrier, count - 1)
+    for piece in carry_pieces(reverse, *refs):
+        piece()
+
+
+def state_back_work(
+    input_ref,
+    grad_ref,
+    carried_ref,
+    decay_ref,
+    weight_ref,
+    skip_ref,
+    input_grad_ref,
+    weight_grad_ref,
+    power_grad_ref,
+    skip_grad_ref,
+    later_ref,
+    ends,
+    outgoing,
+    arrived,
+    joined,
+    final,
+    held,
+    send,
+    receive,
+):
+    carry = carry_pieces(True, grad_ref, decay_ref, later_ref, ends, outgoing, arrived, joined, final, send, receive)
+
+    def tile_piece(tile):
+        cut_at = slice(tile * lanes, (tile + 1) * lanes)
+        wide = (input_ref, grad_ref, carried_ref, later_ref)
+        flat = (decay_ref, weight_ref, skip_ref)
+        results = (weight_grad_ref, power_grad_ref, skip_grad_ref)
+        back_kernel(
+            *(r.at[:, :, cut_at] for r in wide),
+            *(r.at[:, cut_at] for r in flat),
+            input_grad_ref.at[:, :, cut_at],
+            *(r.at[:, cut_at] for r in results),
+            held,
+        )
+
+    tiles = [functools.partial(tile_piece, tile) for tile in range(input_ref.shape[2] // lanes)]
+    return list(carry) + tiles
 
 
 def carried_by_kernel(value, decay, reverse, collective):
@@ -1327,17 +1398,60 @@
     into_gated = into_gated.reshape(seq_count, block_len, model_width)
     query_mixer_grad = into_gated * state_y
     state_grad = into_gated * query_mixer
+    table = shaped(states, model_width)
+    gains_at = 3 * states + reach
+    table_edges = [0, states, 2 * states, 3 * states, gains_at, small_width]
+
+    def tables_of(block):
+        return [block[:, a:b] for a, b in zip(table_edges, table_edges[1:])]
+
+    orders = ("yxz", "xyz", "xzy", "yxz", "xyz", "yzx")
     if by_kernel:
-        later = carried_by_kernel(state_grad, decay, True, 3)
+        main = [attend_inputs_grad, first_up_grad, mixer_output_grad, first_down_grad, attend_output_grad]
+        plan = chunked([g.shape[1] for g in main], (4, 4, 2, 4, 2), orders)
+        part = attend_cols // 3 // groups
+
+        def finish(index, block, results):
+            if index > 0:
+                results[index][...] = block[...]
+                return
+            for group in range(groups):
+                for kind in range(3):
+                    start = (kind * groups + group) * part
+                    source = group * padded + kind * part
+                    results[0][:, start : start + part] = block[:, source : source + part]
+
+        results = [shaped(share, w) for w in (attend_cols, first_up.shape[1], model_width)]
+        results += [shaped(share * fold, model_width), shaped(share, model_width)]
+        parts = pltpu.VMEM((seq_devices, seq_count * states // seq_devices, model_width), bf16)
+        exchange_sems = pltpu.SemaphoreType.DMA((2, seq_devices - 1))
+        work = (
+            state_back_work,
+            (inner, state_grad, carried, decay, weight, skip[None]),
+            (wide, table, table, shaped(1, model_width)),
+            (
+                pltpu.VMEM((seq_count, states, model_width), f32),
+                pltpu.VMEM((seq_count, states, lanes), f32),
+                parts,
+                parts,
+                parts,
+                parts,
+                pltpu.VMEM((block_len, seq_count, states, lanes), f32),
+                exchange_sems,
+                exchange_sems,
+            ),
+        )
+        scattered_main = scatter_blocks(main, plan, finish, results, gap=4, work=work)
+        attend_inputs_out, first_up_out, mixer_output_out, first_down_out, attend_output_out = scattered_main[:5]
+        inner_grad, weight_grad, power_grad, skip_grad = scattered_main[5:]
     else:
         later = carried_in(encode(state_grad, decay, True), decay, block_len, True)
-    table = shaped(states, model_width)
-    inner_grad, weight_grad, power_grad, skip_grad = per_lane_tile(
-        back_kernel,
-        (inner, state_grad, carried, later, decay, weight, skip[None]),
-        (wide, table, table, shaped(1, model_width)),
-        scratch=[pltpu.VMEM((block_len, seq_count, states, lanes), f32)],
-    )
+        inner_grad, weight_grad, power_grad, skip_grad = per_lane_tile(
+            back_kernel,
+            (inner, state_grad, carried, later, decay, weight, skip[None]),
+            (wide, table, table, shaped(1, model_width)),
+            scratch=[pltpu.VMEM((block_len, seq_count, states, lanes), f32)],
+        )
     extended_grad, taps_grad, value_mixer_grad = shift_back(inner_grad)
     spill = passed_along(extended_grad[:, : reach - 1], "seq", -1)
     keys_mixer_grad = extended_grad[:, reach - 1 :] + jnp.pad(
@@ -1364,41 +1478,20 @@
     def unfolded(folded):
         return folded.reshape(share, fold, model_width).transpose(1, 0, 2).reshape(share * fold, model_width)
 
-    gains_at = 3 * states + reach
-    table_edges = [0, states, 2 * states, 3 * states, gains_at, small_width]
-
-    def tables_of(block):
-        return [block[:, a:b] for a, b in zip(table_edges, table_edges[1:])]
-
-    last = [attend_inputs_grad, first_up_grad, mixer_output_grad, mixer_inputs_grad, small_grad]
     if by_kernel:
-        last += [first_down_grad, attend_output_grad]
-        orders = ("yxz", "xyz", "xzy", "yxz", "xyz", "yzx")
-        plan = chunked([g.shape[1] for g in last], (4, 4, 2, 4, 2, 4, 2), orders)
-        part = attend_cols // 3 // groups
-
-        def finish(index, block, results):
-            if index == 0:
-                for group in range(groups):
-                    for kind in range(3):
-                        start = (kind * groups + group) * part
-                        source = group * padded + kind * part
-                        results[0][:, start : start + part] = block[:, source : source + part]
-            elif index == 4:
-                for place, table in enumerate(tables_of(block)):
-                    results[5 + place][...] = table
-            else:
-                results[{1: 1, 2: 2, 3: 3, 5: 4, 6: 10}[index]][...] = block[...]
-
-        widths = [attend_cols] + [g.shape[1] for g in last[1:4]]
-        results = [shaped(share, w) for w in widths] + [shaped(share * fold, model_width)]
+        plan = chunked((mixer_inputs_grad.shape[1], small_width), (4, 2), orders)
+
+        def finish_small(index, block, results):
+            for result, piece in zip(results[1:] if index else results[:1], tables_of(block) if index else [block]):
+                result[...] = piece[...]
+
+        results = [shaped(share, mixer_inputs_grad.shape[1])]
         results += [shaped(share, b - a) for a, b in zip(table_edges, table_edges[1:])]
-        results.append(shaped(share, model_width))
-        attend_inputs_out, first_up_out, mixer_output_out, mixer_inputs_out, first_down_out, *tables = (
-            scatter_blocks(last, plan, finish, results, gap=4)
-        )
-        *tables, attend_output_out = tables
+        mixer_inputs_out, *tables = scatter_blocks(
+            [mixer_inputs_grad, small_grad], plan, finish_small, results, gap=2, collective=4
+        )
     else:
+        last = [attend_inputs_grad, first_up_grad, mixer_output_grad, mixer_inputs_grad, small_grad]
         last += [fold_all(first_down_grad, share, model_width), attend_output_grad]
         *last, folded, attend_output_out = scattered(last)
         first_down_out = unfolded(folded).astype(f32)

time: 563 us -> 575 us (1.021)
  Pallas kernels: 321 us -> 329 us
    pallas_call x1 -> x2, Pallas kernels: 103 us -> 154 us  [scatter_blocks(): pl.pallas_call(functools.partial(scatter_kernel, plan, gap, finish, besid...]
    pallas_call x2 -> x1, Pallas kernels: 51.4 us -> 29.5 us  [carried_by_kernel(): pl.pallas_call(functools.partial(carry_kernel, reverse), out_shape=shaped...]
    pallas_call x2 -> x1, Pallas kernels: 30.1 us -> 9.28 us  [per_lane_tile(): pl.pallas_call(kernel, grid=(args[0].shape[-1] // lanes,), in_specs=[spec...]
    unnamed x169 -> x193, local copies, waits for them, and re-layouts: 26.1 us -> 24.4 us
  transfers between devices with their start and end apart: 7 -> 7, of which waited for: 4 -> 5; matrix products, arithmetic and copies ran while one was open for 9% -> 9% of each run, Pallas kernels for 52% -> 53%
where the time goes in v3:
time: 575 us; the launch traced here: 565 us
  Pallas kernels  329 us (57%)
  blocking collectives  69.5 us (12%)
  waiting for transfers between devices  57.7 us (10%)
  local copies, waits for them, and re-layouts  36.6 us (6%)
  matrix products  26.9 us (5%)
  other arithmetic  17.3 us (3%)
  between operations  15.7 us (3%)
  starting transfers between devices  12.5 us (2%)
    pallas_call x2, Pallas kernels, scatter_blocks(): pl.pallas_call(functools.partial(scatter_kernel, plan, gap, finish, besid...  154 us
    pallas_call x1, Pallas kernels, gather_blocks(): pl.pallas_call(functools.partial(gather_kernel, plan, gap), out_shape=out...  75.8 us
    all_to_all x2, blocking collectives, deal(): lax.all_to_all(parts, 'seq', split_axis=0, concat_axis=0, tiled=True)  69.5 us
    all_to_all x2, waiting for transfers between devices, collect(): back = lax.all_to_all(parts, 'seq', split_axis=0, concat_axis=0, tiled=True)  38.3 us
    pallas_call x1, Pallas kernels, carried_by_kernel(): pl.pallas_call(functools.partial(carry_kernel, reverse), out_shape=shaped...  29.5 us
    pallas_call x2, Pallas kernels, feed_back_blocks(): pl.pallas_call(functools.partial(feed_back_kernel, packed), grid=(inner /...  25.4 us
    unnamed x193, local copies, waits for them, and re-layouts  24.4 us
    all_gather x1, waiting for transfers between devices, body(): lax.all_gather(jnp.concatenate(packed, axis=1), everyone, axis=0, tiled=T...  14.8 us
  transfers between devices with their start and end apart: 7, of which 5 were waited for; matrix products, arithmetic and copies ran while one was open for 9% of the time, Pallas kernels for 53%

profile of v3, /device:TPU:0, one launch (start us, length us, event | category | flops | bytes accessed | tf_op | source)
XLA Modules:
  0.0 565.1 jit_solution(16103297649753118480)
XLA Ops:
  14.6 75.8 %shard_map.339 = (bf16[4,2,2,2,24,2560]{5,4,3,2,1,0:T(8,128)(2,1)}, bf16[4,2,2,2,96,768]{5,4,3,2,1,0:T(8,128)(2,1)}) custom-call(bf16[24,2560]{1,0:T(8,128)(2,1)} %fusion.22.refs_0_, bf16[96,768]{1,0:T(8,128)(2,1)} %refs_1_.1), custom_call_target="tpu_custom_call" | custom-call | bytes 17301504 | tf_op jit(solution)/shard_map/pallas_call | solution.py:307
  92.7 3.4 fusion
  101.1 29.5 %shard_map.340.carried_ref.refs_7_ = f32[2,64,768]{2,1,0:T(8,128)} custom-call(f32[2,128,768]{2,1,0:T(8,128)} %get-tuple-element.161.refs_0_.input_ref.refs_5_, f32[64,768]{1,0:T(8,128)} %get-tuple-element.186.refs_1_.decay_ref.refs_8_), custom_call_target="tpu_custom_call" | custom-call | bytes 6291456 | tf_op jit(solution)/shard_map/pallas_call | solution.py:603
  132.8 9.3 %shard_map.341 = (f32[2,128,768]{2,1,0:T(8,128)S(1)}, f32[2,128,768]{2,1,0:T(8,128)S(1)}) custom-call(f32[2,128,768]{2,1,0:T(8,128)S(1)} %copy-done.2, f32[2,128,768]{2,1,0:T(8,128)S(1)} %get-tuple-element.163.query_ref, f32[2,64,768]{2,1,0:T(8,128)S(1)} %copy-done.3, f32[64,768]{1,0:T(8,128)S(1)} %copy-done.4, ...), custom_call_target="tpu_custom_call" | custom-call | bytes 2362368 | tf_op jit(solution)/shard_map/pallas_call | solution.py:154
  143.1 14.8 %all-gather.3.cloned.1.call-done.up_ref = bf16[768,10240]{1,0:T(8,128)(2,1)} async-done(((bf16[24,10240]{1,0:T(8,128)(2,1)}), bf16[768,10240]{1,0:T(8,128)(2,1)}) %all-gather.3.cloned.1.call-update) | async-done | bytes 15728656 | tf_op jit(solution)/shard_map/all_gather | solution.py:1258
  162.0 5.9 %shard_map.342 = (f32[256,768]{1,0:T(8,128)S(1)}, bf16[256,768]{1,0:T(8,128)(2,1)S(1)}, bf16[256,3072]{1,0:T(8,128)(2,1)S(1)}, bf16[256,3072]{1,0:T(8,128)(2,1)S(1)}) custom-call(f32[256,768]{1,0:T(8,128)S(1)} %convolution_add_fusion.1.resid_ref, f32[1,768]{1,0:T(1,128)S(1)} %get-tuple-element.183.gain_ref, ...), custom_call_target="tpu_custom_call" | custom-call | flops 2415919104 | bytes 23592960 | tf_op jit(solution)/shard_map/pallas_call | solution.py:642
  170.6 3.4 convolution_convert_fusion.2
  174.5 52.6 %all_to_all.20 = bf16[8,128,640]{2,1,0:T(8,128)(2,1)} all-to-all(bf16[8,128,640]{2,1,0:T(8,128)(2,1)S(1)} %bitcast.118), channel_id=1, replica_groups=mesh['seq'=8,'batch'=4] {'seq'}, dimensions={0} | all-to-all | bytes 2621440 | tf_op jit(solution)/shard_map/all_to_all | solution.py:1328
  227.1 11.0 %shard_map.343 = (bf16[1024,256]{1,0:T(8,128)(2,1)}, f32[1024,192]{1,0:T(8,128)}, f32[3,1024,128]{2,1,0:T(8,128)}) custom-call(bf16[1024,640]{1,0:T(8,128)(2,1)} %bitcast.113), custom_call_target="tpu_custom_call" | custom-call | tf_op jit(solution)/shard_map/pallas_call | solution.py:890
  238.1 4.1 all-to-all-start.1
  244.4 10.0 %all-to-all-done.1 = bf16[8,128,256]{2,1,0:T(8,128)(2,1)} async-done(((bf16[8,128,256]{2,1,0:T(8,128)(2,1)}), bf16[8,128,256]{2,1,0:T(8,128)(2,1)}, u32[]{:S(2)}, u32[]{:S(2)}) %all-to-all-start.1) | async-done | bytes 524320 | tf_op jit(solution)/shard_map/all_to_all | solution.py:1333
  260.2 5.9 %shard_map.344 = (f32[256,768]{1,0:T(8,128)S(1)}, bf16[256,768]{1,0:T(8,128)(2,1)S(1)}, bf16[256,3072]{1,0:T(8,128)(2,1)S(1)}, bf16[256,3072]{1,0:T(8,128)(2,1)S(1)}) custom-call(f32[256,768]{1,0:T(8,128)S(1)} %convolution_add_fusion.resid_ref, f32[1,768]{1,0:T(1,128)S(1)} %get-tuple-element.182.gain_ref, ...), custom_call_target="tpu_custom_call" | custom-call | flops 2415919104 | bytes 23592960 | tf_op jit(solution)/shard_map/pallas_call | solution.py:642
  267.1 12.9 %shard_map.345 = (f32[256,768]{1,0:T(8,128)S(1)}, f32[1,768]{1,0:T(1,128)S(1)}, bf16[768,6144]{1,0:T(8,128)(2,1)}) custom-call(f32[256,768]{1,0:T(8,128)S(1)} %bitcast.110, f32[256,768]{1,0:T(8,128)S(1)} %convolution_add_fusion.resid_ref, f32[1,768]{1,0:T(1,128)S(1)} %get-tuple-element.182.gain_ref, bf16[256,768]{1,0:T(8,128)(2,1)S(1)} %get-tuple-element.68.normed_ref, ...), custom_call_target="tpu_custom_call" | custom-call | flops 4831838208 | bytes 37748736 | tf_op jit(solution)/shard_map/pallas_call | solution.py:779
  280.8 16.9 %all_to_all.21 = bf16[8,128,256]{2,1,0:T(8,128)(2,1)} all-to-all(bf16[8,128,256]{2,1,0:T(8,128)(2,1)S(1)} %bitcast.129), channel_id=1, replica_groups=mesh['seq'=8,'batch'=4] {'seq'}, dimensions={0} | all-to-all | bytes 1048576 | tf_op jit(solution)/shard_map/all_to_all | solution.py:1328
  297.7 12.4 %shard_map.346 = bf16[1024,640]{1,0:T(8,128)(2,1)} custom-call(bf16[1024,640]{1,0:T(8,128)(2,1)} %bitcast.114, bf16[1024,256]{1,0:T(8,128)(2,1)} %bitcast.131, f32[1024,192]{1,0:T(8,128)} %get-tuple-element.72.full_ref, f32[3,1024,128]{2,1,0:T(8,128)} %get-tuple-element.73.stat_ref), custom_call_target="tpu_custom_call" | custom-call | tf_op jit(solution)/shard_map/pallas_call | solution.py:907
  310.2 4.6 all-to-all-start.3
  317.2 28.2 %all-to-all-done.3 = bf16[8,128,640]{2,1,0:T(8,128)(2,1)} async-done(((bf16[8,128,640]{2,1,0:T(8,128)(2,1)}), bf16[8,128,640]{2,1,0:T(8,128)(2,1)}, u32[]{:S(2)}, u32[]{:S(2)}) %all-to-all-start.3) | async-done | bytes 1310752 | tf_op jit(solution)/shard_map/all_to_all | solution.py:1333
  346.9 4.2 multiply_reduce_fusion
  353.1 12.5 %shard_map.347 = (f32[256,768]{1,0:T(8,128)S(1)}, f32[1,768]{1,0:T(1,128)S(1)}, bf16[768,3072]{1,0:T(8,128)(2,1)}, bf16[3072,768]{1,0:T(8,128)(2,1)}) custom-call(f32[256,768]{1,0:T(8,128)S(1)} %add_add_fusion.2.upstream_ref, f32[256,768]{1,0:T(8,128)S(1)} %convolution_add_fusion.1.resid_ref, f32[1,768]{1,0:T(1,128)S(1)} %get-tuple-element.183.gain_ref, ...), custom_call_target="tpu_custom_call" | custom-call | flops 4831838208 | bytes 37748736 | tf_op jit(solution)/shard_map/pallas_call | solution.py:779
  371.3 3.3 convolution_convert_fusion.1
  374.6 116.6 %shard_map.348 = (f32[24,2304]{1,0:T(8,128)}, f32[24,3072]{1,0:T(8,128)}, f32[24,768]{1,0:T(8,128)}, f32[96,768]{1,0:T(8,128)}, f32[24,768]{1,0:T(8,128)}, /*ind...) custom-call(bf16[4,2,2,2,24,2560]{5,4,3,2,1,0:T(8,128)(2,1)} %bitcast.124, ...), custom_call_target="tpu_custom_call" | custom-call | bytes 62914560 | tf_op jit(solution)/shard_map/pallas_call | solution.py:453
  495.5 4.0 collective-permute-done.1
  505.6 2.9 convolution_convert_fusion
  508.5 37.0 %shard_map.349 = (f32[24,2304]{1,0:T(8,128)}, f32[24,64]{1,0:T(8,128)}, f32[24,64]{1,0:T(8,128)}, f32[24,64]{1,0:T(8,128)}, f32[24,4]{1,0:T(8,128)}, /*index=5*/f32[24,60]{1,0:T(8,128)}) custom-call(bf16[4,2,2,2,24,2304]{5,4,3,2,1,0:T(8,128)(2,1)} %bitcast.125, bf16[4,2,2,2,24,256]{5,4,3,2,1,0:T(8,128)(2,1)} %bitcast.132), custom_call_target="tpu_custom_call" | custom-call | bytes 15728640 | tf_op jit(solution)/shard_map/pallas_call | solution.py:453
  (289 shorter events, 68.0 us)
Async XLA Ops:
  7.3 150.5 %all-gather.3.cloned.1.call-start = ((), (), s32[]{:S(2)}) async-start(), calls=%async_computation.5 | async-start | bytes 16220160 | tf_op jit(solution)/shard_map/all_gather | solution.py:1258
  8.7 82.9 %copy-start.13 = (bf16[2,128,768]{2,1,0:T(8,128)(2,1)S(1)}, bf16[2,128,768]{2,1,0:T(8,128)(2,1)}, u32[]{:S(2)}) copy-start(bf16[2,128,768]{2,1,0:T(8,128)(2,1)} %param.20) | copy-start | bytes 1179652
  13.1 244.7 %all-gather.5.cloned.1.call-start = ((), (), s32[]{:S(2)}) async-start(), calls=%async_computation.6 | async-start | bytes 4866048 | tf_op jit(solution)/shard_map/all_gather | solution.py:1264
  92.7 37.9 %copy-start.12 = (f32[1,768]{1,0:T(1,128)}, f32[1,768]{1,0:T(1,128)S(1)}, u32[]{:S(2)}) copy-start(f32[1,768]{1,0:T(1,128)S(1)} %get-tuple-element.184.skip_ref.refs_10_) | copy-start | bytes 9220
  92.7 77.9 %copy-start.58 = (f32[768]{0:T(1024)}, f32[768]{0:T(1024)S(1)}, u32[]{:S(2)}) copy-start(f32[768]{0:T(1024)S(1)} %get-tuple-element.147) | copy-start | bytes 9220
  96.2 3.4 collective-permute-start
  98.8 31.9 %copy-start.5 = (f32[64,768]{1,0:T(8,128)}, f32[64,768]{1,0:T(8,128)S(1)}, u32[]{:S(2)}) copy-start(f32[64,768]{1,0:T(8,128)S(1)} %get-tuple-element.185.weight_ref.refs_9_) | copy-start | bytes 589828
  99.5 31.1 %copy-start.4 = (f32[64,768]{1,0:T(8,128)S(1)}, f32[64,768]{1,0:T(8,128)}, u32[]{:S(2)}) copy-start(f32[64,768]{1,0:T(8,128)} %get-tuple-element.186.refs_1_.decay_ref.refs_8_) | copy-start | bytes 589828
  143.1 16.6 %copy-start.22 = (bf16[2,128,768]{2,1,0:T(8,128)(2,1)}, bf16[2,128,768]{2,1,0:T(8,128)(2,1)S(1)}, u32[]{:S(2)}) copy-start(bf16[2,128,768]{2,1,0:T(8,128)(2,1)S(1)} %convert_element_type.109) | copy-start | bytes 1179652
  174.5 68.0 %copy-start.82 = (s32[2]{0:T(128)S(1)}, s32[2]{0:T(128)}, u32[]{:S(2)}) copy-start(s32[2]{0:T(128)} %param.22) | copy-start | bytes 28
  227.1 16.0 %slice-start = ((bf16[768,10240]{1,0:T(8,128)(2,1)}), bf16[768,768]{1,0:T(8,128)(2,1)S(1)}, s32[]{:S(2)}) async-start(bf16[768,10240]{1,0:T(8,128)(2,1)} %all-gather.3.cloned.1.call-done.up_ref), calls=%async_computation.8 | async-start | bytes 2359296 | tf_op jit(solution)/shard_map/slice | solution.py:1186
  238.1 16.3 %all-to-all-start.1 = ((bf16[8,128,256]{2,1,0:T(8,128)(2,1)}), bf16[8,128,256]{2,1,0:T(8,128)(2,1)}, u32[]{:S(2)}, u32[]{:S(2)}) async-start(bf16[8,128,256]{2,1,0:T(8,128)(2,1)} %bitcast.137), calls=%async_computation.1 | async-start | bytes 1048576 | tf_op jit(solution)/shard_map/all_to_all | solution.py:1333
  242.3 306.4 %reduce-scatter.2.cloned.1.call-start = ((), (), s32[]{:S(2)}) async-start(), calls=%async_computation.7 | async-start | bytes 9732096 | tf_op jit(solution)/shard_map/reduce_scatter | solution.py:1384
  267.1 12.9 %copy-start.19 = (bf16[4,256,768]{2,1,0:T(8,128)(2,1)S(1)}, bf16[4,256,768]{2,1,0:T(8,128)(2,1)}, u32[]{:S(2)}) copy-start(bf16[4,256,768]{2,1,0:T(8,128)(2,1)} %pad.47) | copy-start | bytes 4718596
  310.2 35.2 %all-to-all-start.3 = ((bf16[8,128,640]{2,1,0:T(8,128)(2,1)}), bf16[8,128,640]{2,1,0:T(8,128)(2,1)}, u32[]{:S(2)}, u32[]{:S(2)}) async-start(bf16[8,128,640]{2,1,0:T(8,128)(2,1)} %bitcast.119), calls=%async_computation.3 | async-start | bytes 2621440 | tf_op jit(solution)/shard_map/all_to_all | solution.py:1333
  316.0 30.9 %copy-start.59 = (f32[768]{0:T(1024)S(1)}, f32[768]{0:T(1024)}, u32[]{:S(2)}) copy-start(f32[768]{0:T(1024)} %copy-done.58) | copy-start | bytes 9220
  316.1 30.9 %copy-start.66 = (f32[256]{0:T(256)S(1)}, f32[256]{0:T(256)}, u32[]{:S(2)}) copy-start(f32[256]{0:T(256)} %copy-done.65) | copy-start | bytes 3076
  316.1 30.9 %copy-start.77 = (f32[256]{0:T(256)S(1)}, f32[256]{0:T(256)}, u32[]{:S(2)}) copy-start(f32[256]{0:T(256)} %copy-done.76) | copy-start | bytes 3076
  353.1 12.5 %copy-start.23 = (bf16[2,128,768]{2,1,0:T(8,128)(2,1)S(1)}, bf16[2,128,768]{2,1,0:T(8,128)(2,1)}, u32[]{:S(2)}) copy-start(bf16[2,128,768]{2,1,0:T(8,128)(2,1)} %copy-done.22) | copy-start | bytes 1179652
  374.6 116.6 %copy-start.16 = (f32[2,128,2304]{2,1,0:T(8,128)S(1)}, f32[2,128,2304]{2,1,0:T(8,128)}, u32[]{:S(2)}) copy-start(f32[2,128,2304]{2,1,0:T(8,128)} %copy-done.15) | copy-start | bytes 7077892
  374.6 116.6 %copy-start.18 = (f32[2,128,768]{2,1,0:T(8,128)S(1)}, f32[2,128,768]{2,1,0:T(8,128)}, u32[]{:S(2)}) copy-start(f32[2,128,768]{2,1,0:T(8,128)} %copy-done.17) | copy-start | bytes 2359300
  374.6 116.6 %copy-start.46 = (f32[2,3,768]{2,1,0:T(4,128)S(1)}, f32[2,3,768]{2,1,0:T(4,128)}, u32[]{:S(2)}) copy-start(f32[2,3,768]{2,1,0:T(4,128)} %copy-done.45) | copy-start | bytes 55300
  493.5 6.0 %collective-permute-start.1 = (f32[2,3,768]{2,1,0:T(4,128)S(1)}, f32[2,3,768]{2,1,0:T(4,128)S(1)}, u32[]{:S(2)}, u32[]{:S(2)}) collective-permute-start(f32[2,3,768]{2,1,0:T(4,128)S(1)} %pad_add_fusion.1), channel_id=1, source_target_pairs={{4,0},{8,4},{12,8},{16,12},{20,16},{24,20},{28,24},{5,1},{9,5},{13... | collective-permute-start | bytes 55304 | tf_op jit(solution)/shard_map/ppermute | solution.py:183
  508.5 46.3 %copy-start.48 = (f32[24,768]{1,0:T(8,128)S(1)}, f32[24,768]{1,0:T(8,128)}, u32[]{:S(2)}) copy-start(f32[24,768]{1,0:T(8,128)} %get-tuple-element.236) | copy-start | bytes 221188
  (72 other events, 294.5 us)
Sparse Core Ops, SparseCore 0:
  13.2 144.5 all-gather.2
  160.7 69.7 all-gather.4
  310.2 163.9 reduce-scatter.1

commit v4 on v3

--- a/solution.py
+++ b/solution.py
@@ -361,7 +361,7 @@
 
     steps, pieces = list(staggered(len(plan), 4, gap)), len(work)
     for turn, (stage, chunk) in enumerate(steps):
-        while work and turn * pieces >= (pieces - len(work)) * len(steps) * 3 // 4:
+        while work and turn >= work_starts[pieces - len(work)] * len(steps) // 100:
             work.pop(0)()
         index, first, width, order = plan[chunk]
         x_first, line_last = order[0] == "y", order[-1] == "z"
@@ -553,6 +553,9 @@
     pl.semaphore_wait(barrier, count - 1)
     for piece in carry_pieces(reverse, *refs):
         piece()
+
+
+work_starts = (0, 22, 40, 45, 51, 57, 63, 69, 75)
 
 
 def state_back_work(

time: 575 us -> 575 us (level)
  no operation moved by 1% of the time
where the time goes in v4:
time: 575 us; the launch traced here: 565 us
  Pallas kernels  329 us (57%)
  blocking collectives  69.5 us (12%)
  waiting for transfers between devices  57.7 us (10%)
  local copies, waits for them, and re-layouts  36.6 us (6%)
  matrix products  26.9 us (5%)
  other arithmetic  17.3 us (3%)
  between operations  15.7 us (3%)
  starting transfers between devices  12.5 us (2%)
    pallas_call x2, Pallas kernels, scatter_blocks(): pl.pallas_call(functools.partial(scatter_kernel, plan, gap, finish, besid...  154 us
    pallas_call x1, Pallas kernels, gather_blocks(): pl.pallas_call(functools.partial(gather_kernel, plan, gap), out_shape=out...  75.8 us
    all_to_all x2, blocking collectives, deal(): lax.all_to_all(parts, 'seq', split_axis=0, concat_axis=0, tiled=True)  69.5 us
    all_to_all x2, waiting for transfers between devices, collect(): back = lax.all_to_all(parts, 'seq', split_axis=0, concat_axis=0, tiled=True)  38.3 us
    pallas_call x1, Pallas kernels, carried_by_kernel(): pl.pallas_call(functools.partial(carry_kernel, reverse), out_shape=shaped...  29.5 us
    pallas_call x2, Pallas kernels, feed_back_blocks(): pl.pallas_call(functools.partial(feed_back_kernel, packed), grid=(inner /...  25.4 us
    unnamed x193, local copies, waits for them, and re-layouts  24.4 us
    all_gather x1, waiting for transfers between devices, body(): lax.all_gather(jnp.concatenate(packed, axis=1), everyone, axis=0, tiled=T...  14.8 us
  transfers between devices with their start and end apart: 7, of which 5 were waited for; matrix products, arithmetic and copies ran while one was open for 9% of the time, Pallas kernels for 53%

profile of v4, /device:TPU:0, one launch (start us, length us, event | category | flops | bytes accessed | tf_op | source)
XLA Modules:
  0.0 565.2 jit_solution(7542793917943557078)
XLA Ops:
  14.6 75.8 %shard_map.339 = (bf16[4,2,2,2,24,2560]{5,4,3,2,1,0:T(8,128)(2,1)}, bf16[4,2,2,2,96,768]{5,4,3,2,1,0:T(8,128)(2,1)}) custom-call(bf16[24,2560]{1,0:T(8,128)(2,1)} %fusion.22.refs_0_, bf16[96,768]{1,0:T(8,128)(2,1)} %refs_1_.1), custom_call_target="tpu_custom_call" | custom-call | bytes 17301504 | tf_op jit(solution)/shard_map/pallas_call | solution.py:307
  92.7 3.4 fusion
  101.1 29.5 %shard_map.340.carried_ref.refs_7_ = f32[2,64,768]{2,1,0:T(8,128)} custom-call(f32[2,128,768]{2,1,0:T(8,128)} %get-tuple-element.161.refs_0_.input_ref.refs_5_, f32[64,768]{1,0:T(8,128)} %get-tuple-element.186.refs_1_.decay_ref.refs_8_), custom_call_target="tpu_custom_call" | custom-call | bytes 6291456 | tf_op jit(solution)/shard_map/pallas_call | solution.py:606
  132.8 9.3 %shard_map.341 = (f32[2,128,768]{2,1,0:T(8,128)S(1)}, f32[2,128,768]{2,1,0:T(8,128)S(1)}) custom-call(f32[2,128,768]{2,1,0:T(8,128)S(1)} %copy-done.2, f32[2,128,768]{2,1,0:T(8,128)S(1)} %get-tuple-element.163.query_ref, f32[2,64,768]{2,1,0:T(8,128)S(1)} %copy-done.3, f32[64,768]{1,0:T(8,128)S(1)} %copy-done.4, ...), custom_call_target="tpu_custom_call" | custom-call | bytes 2362368 | tf_op jit(solution)/shard_map/pallas_call | solution.py:154
  143.1 14.8 %all-gather.3.cloned.1.call-done.up_ref = bf16[768,10240]{1,0:T(8,128)(2,1)} async-done(((bf16[24,10240]{1,0:T(8,128)(2,1)}), bf16[768,10240]{1,0:T(8,128)(2,1)}) %all-gather.3.cloned.1.call-update) | async-done | bytes 15728656 | tf_op jit(solution)/shard_map/all_gather | solution.py:1261
  162.0 5.9 %shard_map.342 = (f32[256,768]{1,0:T(8,128)S(1)}, bf16[256,768]{1,0:T(8,128)(2,1)S(1)}, bf16[256,3072]{1,0:T(8,128)(2,1)S(1)}, bf16[256,3072]{1,0:T(8,128)(2,1)S(1)}) custom-call(f32[256,768]{1,0:T(8,128)S(1)} %convolution_add_fusion.1.resid_ref, f32[1,768]{1,0:T(1,128)S(1)} %get-tuple-element.183.gain_ref, ...), custom_call_target="tpu_custom_call" | custom-call | flops 2415919104 | bytes 23592960 | tf_op jit(solution)/shard_map/pallas_call | solution.py:645
  170.6 3.4 convolution_convert_fusion.2
  174.5 52.6 %all_to_all.20 = bf16[8,128,640]{2,1,0:T(8,128)(2,1)} all-to-all(bf16[8,128,640]{2,1,0:T(8,128)(2,1)S(1)} %bitcast.118), channel_id=1, replica_groups=mesh['seq'=8,'batch'=4] {'seq'}, dimensions={0} | all-to-all | bytes 2621440 | tf_op jit(solution)/shard_map/all_to_all | solution.py:1331
  227.1 11.0 %shard_map.343 = (bf16[1024,256]{1,0:T(8,128)(2,1)}, f32[1024,192]{1,0:T(8,128)}, f32[3,1024,128]{2,1,0:T(8,128)}) custom-call(bf16[1024,640]{1,0:T(8,128)(2,1)} %bitcast.113), custom_call_target="tpu_custom_call" | custom-call | tf_op jit(solution)/shard_map/pallas_call | solution.py:893
  238.1 4.1 all-to-all-start.1
  244.4 10.0 %all-to-all-done.1 = bf16[8,128,256]{2,1,0:T(8,128)(2,1)} async-done(((bf16[8,128,256]{2,1,0:T(8,128)(2,1)}), bf16[8,128,256]{2,1,0:T(8,128)(2,1)}, u32[]{:S(2)}, u32[]{:S(2)}) %all-to-all-start.1) | async-done | bytes 524320 | tf_op jit(solution)/shard_map/all_to_all | solution.py:1336
  260.2 5.9 %shard_map.344 = (f32[256,768]{1,0:T(8,128)S(1)}, bf16[256,768]{1,0:T(8,128)(2,1)S(1)}, bf16[256,3072]{1,0:T(8,128)(2,1)S(1)}, bf16[256,3072]{1,0:T(8,128)(2,1)S(1)}) custom-call(f32[256,768]{1,0:T(8,128)S(1)} %convolution_add_fusion.resid_ref, f32[1,768]{1,0:T(1,128)S(1)} %get-tuple-element.182.gain_ref, ...), custom_call_target="tpu_custom_call" | custom-call | flops 2415919104 | bytes 23592960 | tf_op jit(solution)/shard_map/pallas_call | solution.py:645
  267.1 12.9 %shard_map.345 = (f32[256,768]{1,0:T(8,128)S(1)}, f32[1,768]{1,0:T(1,128)S(1)}, bf16[768,6144]{1,0:T(8,128)(2,1)}) custom-call(f32[256,768]{1,0:T(8,128)S(1)} %bitcast.110, f32[256,768]{1,0:T(8,128)S(1)} %convolution_add_fusion.resid_ref, f32[1,768]{1,0:T(1,128)S(1)} %get-tuple-element.182.gain_ref, bf16[256,768]{1,0:T(8,128)(2,1)S(1)} %get-tuple-element.68.normed_ref, ...), custom_call_target="tpu_custom_call" | custom-call | flops 4831838208 | bytes 37748736 | tf_op jit(solution)/shard_map/pallas_call | solution.py:782
  280.8 16.9 %all_to_all.21 = bf16[8,128,256]{2,1,0:T(8,128)(2,1)} all-to-all(bf16[8,128,256]{2,1,0:T(8,128)(2,1)S(1)} %bitcast.129), channel_id=1, replica_groups=mesh['seq'=8,'batch'=4] {'seq'}, dimensions={0} | all-to-all | bytes 1048576 | tf_op jit(solution)/shard_map/all_to_all | solution.py:1331
  297.7 12.4 %shard_map.346 = bf16[1024,640]{1,0:T(8,128)(2,1)} custom-call(bf16[1024,640]{1,0:T(8,128)(2,1)} %bitcast.114, bf16[1024,256]{1,0:T(8,128)(2,1)} %bitcast.131, f32[1024,192]{1,0:T(8,128)} %get-tuple-element.72.full_ref, f32[3,1024,128]{2,1,0:T(8,128)} %get-tuple-element.73.stat_ref), custom_call_target="tpu_custom_call" | custom-call | tf_op jit(solution)/shard_map/pallas_call | solution.py:910
  310.2 4.6 all-to-all-start.3
  317.2 28.2 %all-to-all-done.3 = bf16[8,128,640]{2,1,0:T(8,128)(2,1)} async-done(((bf16[8,128,640]{2,1,0:T(8,128)(2,1)}), bf16[8,128,640]{2,1,0:T(8,128)(2,1)}, u32[]{:S(2)}, u32[]{:S(2)}) %all-to-all-start.3) | async-done | bytes 1310752 | tf_op jit(solution)/shard_map/all_to_all | solution.py:1336
  346.9 4.2 multiply_reduce_fusion
  353.1 12.5 %shard_map.347 = (f32[256,768]{1,0:T(8,128)S(1)}, f32[1,768]{1,0:T(1,128)S(1)}, bf16[768,3072]{1,0:T(8,128)(2,1)}, bf16[3072,768]{1,0:T(8,128)(2,1)}) custom-call(f32[256,768]{1,0:T(8,128)S(1)} %add_add_fusion.2.upstream_ref, f32[256,768]{1,0:T(8,128)S(1)} %convolution_add_fusion.1.resid_ref, f32[1,768]{1,0:T(1,128)S(1)} %get-tuple-element.183.gain_ref, ...), custom_call_target="tpu_custom_call" | custom-call | flops 4831838208 | bytes 37748736 | tf_op jit(solution)/shard_map/pallas_call | solution.py:782
  371.3 3.3 convolution_convert_fusion.1
  374.6 116.6 %shard_map.348 = (f32[24,2304]{1,0:T(8,128)}, f32[24,3072]{1,0:T(8,128)}, f32[24,768]{1,0:T(8,128)}, f32[96,768]{1,0:T(8,128)}, f32[24,768]{1,0:T(8,128)}, /*ind...) custom-call(bf16[4,2,2,2,24,2560]{5,4,3,2,1,0:T(8,128)(2,1)} %bitcast.124, ...), custom_call_target="tpu_custom_call" | custom-call | bytes 62914560 | tf_op jit(solution)/shard_map/pallas_call | solution.py:453
  495.6 4.0 collective-permute-done.1
  505.6 2.9 convolution_convert_fusion
  508.5 37.1 %shard_map.349 = (f32[24,2304]{1,0:T(8,128)}, f32[24,64]{1,0:T(8,128)}, f32[24,64]{1,0:T(8,128)}, f32[24,64]{1,0:T(8,128)}, f32[24,4]{1,0:T(8,128)}, /*index=5*/f32[24,60]{1,0:T(8,128)}) custom-call(bf16[4,2,2,2,24,2304]{5,4,3,2,1,0:T(8,128)(2,1)} %bitcast.125, bf16[4,2,2,2,24,256]{5,4,3,2,1,0:T(8,128)(2,1)} %bitcast.132), custom_call_target="tpu_custom_call" | custom-call | bytes 15728640 | tf_op jit(solution)/shard_map/pallas_call | solution.py:453
  (289 shorter events, 68.0 us)
Async XLA Ops:
  7.3 150.5 %all-gather.3.cloned.1.call-start = ((), (), s32[]{:S(2)}) async-start(), calls=%async_computation.5 | async-start | bytes 16220160 | tf_op jit(solution)/shard_map/all_gather | solution.py:1261
  8.7 82.9 %copy-start.13 = (bf16[2,128,768]{2,1,0:T(8,128)(2,1)S(1)}, bf16[2,128,768]{2,1,0:T(8,128)(2,1)}, u32[]{:S(2)}) copy-start(bf16[2,128,768]{2,1,0:T(8,128)(2,1)} %param.20) | copy-start | bytes 1179652
  13.1 244.7 %all-gather.5.cloned.1.call-start = ((), (), s32[]{:S(2)}) async-start(), calls=%async_computation.6 | async-start | bytes 4866048 | tf_op jit(solution)/shard_map/all_gather | solution.py:1267
  92.7 37.9 %copy-start.12 = (f32[1,768]{1,0:T(1,128)}, f32[1,768]{1,0:T(1,128)S(1)}, u32[]{:S(2)}) copy-start(f32[1,768]{1,0:T(1,128)S(1)} %get-tuple-element.184.skip_ref.refs_10_) | copy-start | bytes 9220
  92.7 77.9 %copy-start.58 = (f32[768]{0:T(1024)}, f32[768]{0:T(1024)S(1)}, u32[]{:S(2)}) copy-start(f32[768]{0:T(1024)S(1)} %get-tuple-element.147) | copy-start | bytes 9220
  96.2 3.4 collective-permute-start
  98.8 31.9 %copy-start.5 = (f32[64,768]{1,0:T(8,128)}, f32[64,768]{1,0:T(8,128)S(1)}, u32[]{:S(2)}) copy-start(f32[64,768]{1,0:T(8,128)S(1)} %get-tuple-element.185.weight_ref.refs_9_) | copy-start | bytes 589828
  99.5 31.1 %copy-start.4 = (f32[64,768]{1,0:T(8,128)S(1)}, f32[64,768]{1,0:T(8,128)}, u32[]{:S(2)}) copy-start(f32[64,768]{1,0:T(8,128)} %get-tuple-element.186.refs_1_.decay_ref.refs_8_) | copy-start | bytes 589828
  143.1 16.6 %copy-start.22 = (bf16[2,128,768]{2,1,0:T(8,128)(2,1)}, bf16[2,128,768]{2,1,0:T(8,128)(2,1)S(1)}, u32[]{:S(2)}) copy-start(bf16[2,128,768]{2,1,0:T(8,128)(2,1)S(1)} %convert_element_type.109) | copy-start | bytes 1179652
  174.5 68.0 %copy-start.82 = (s32[2]{0:T(128)S(1)}, s32[2]{0:T(128)}, u32[]{:S(2)}) copy-start(s32[2]{0:T(128)} %param.22) | copy-start | bytes 28
  227.1 16.0 %slice-start = ((bf16[768,10240]{1,0:T(8,128)(2,1)}), bf16[768,768]{1,0:T(8,128)(2,1)S(1)}, s32[]{:S(2)}) async-start(bf16[768,10240]{1,0:T(8,128)(2,1)} %all-gather.3.cloned.1.call-done.up_ref), calls=%async_computation.8 | async-start | bytes 2359296 | tf_op jit(solution)/shard_map/slice | solution.py:1189
  238.1 16.3 %all-to-all-start.1 = ((bf16[8,128,256]{2,1,0:T(8,128)(2,1)}), bf16[8,128,256]{2,1,0:T(8,128)(2,1)}, u32[]{:S(2)}, u32[]{:S(2)}) async-start(bf16[8,128,256]{2,1,0:T(8,128)(2,1)} %bitcast.137), calls=%async_computation.1 | async-start | bytes 1048576 | tf_op jit(solution)/shard_map/all_to_all | solution.py:1336
  242.3 306.5 %reduce-scatter.2.cloned.1.call-start = ((), (), s32[]{:S(2)}) async-start(), calls=%async_computation.7 | async-start | bytes 9732096 | tf_op jit(solution)/shard_map/reduce_scatter | solution.py:1387
  267.1 12.9 %copy-start.19 = (bf16[4,256,768]{2,1,0:T(8,128)(2,1)S(1)}, bf16[4,256,768]{2,1,0:T(8,128)(2,1)}, u32[]{:S(2)}) copy-start(bf16[4,256,768]{2,1,0:T(8,128)(2,1)} %pad.47) | copy-start | bytes 4718596
  310.2 35.2 %all-to-all-start.3 = ((bf16[8,128,640]{2,1,0:T(8,128)(2,1)}), bf16[8,128,640]{2,1,0:T(8,128)(2,1)}, u32[]{:S(2)}, u32[]{:S(2)}) async-start(bf16[8,128,640]{2,1,0:T(8,128)(2,1)} %bitcast.119), calls=%async_computation.3 | async-start | bytes 2621440 | tf_op jit(solution)/shard_map/all_to_all | solution.py:1336
  316.0 30.9 %copy-start.59 = (f32[768]{0:T(1024)S(1)}, f32[768]{0:T(1024)}, u32[]{:S(2)}) copy-start(f32[768]{0:T(1024)} %copy-done.58) | copy-start | bytes 9220
  316.1 30.9 %copy-start.66 = (f32[256]{0:T(256)S(1)}, f32[256]{0:T(256)}, u32[]{:S(2)}) copy-start(f32[256]{0:T(256)} %copy-done.65) | copy-start | bytes 3076
  316.1 30.9 %copy-start.77 = (f32[256]{0:T(256)S(1)}, f32[256]{0:T(256)}, u32[]{:S(2)}) copy-start(f32[256]{0:T(256)} %copy-done.76) | copy-start | bytes 3076
  353.1 12.5 %copy-start.23 = (bf16[2,128,768]{2,1,0:T(8,128)(2,1)S(1)}, bf16[2,128,768]{2,1,0:T(8,128)(2,1)}, u32[]{:S(2)}) copy-start(bf16[2,128,768]{2,1,0:T(8,128)(2,1)} %copy-done.22) | copy-start | bytes 1179652
  374.6 116.6 %copy-start.16 = (f32[2,128,2304]{2,1,0:T(8,128)S(1)}, f32[2,128,2304]{2,1,0:T(8,128)}, u32[]{:S(2)}) copy-start(f32[2,128,2304]{2,1,0:T(8,128)} %copy-done.15) | copy-start | bytes 7077892
  374.6 116.6 %copy-start.18 = (f32[2,128,768]{2,1,0:T(8,128)S(1)}, f32[2,128,768]{2,1,0:T(8,128)}, u32[]{:S(2)}) copy-start(f32[2,128,768]{2,1,0:T(8,128)} %copy-done.17) | copy-start | bytes 2359300
  374.6 116.6 %copy-start.46 = (f32[2,3,768]{2,1,0:T(4,128)S(1)}, f32[2,3,768]{2,1,0:T(4,128)}, u32[]{:S(2)}) copy-start(f32[2,3,768]{2,1,0:T(4,128)} %copy-done.45) | copy-start | bytes 55300
  493.6 6.0 %collective-permute-start.1 = (f32[2,3,768]{2,1,0:T(4,128)S(1)}, f32[2,3,768]{2,1,0:T(4,128)S(1)}, u32[]{:S(2)}, u32[]{:S(2)}) collective-permute-start(f32[2,3,768]{2,1,0:T(4,128)S(1)} %pad_add_fusion.1), channel_id=1, source_target_pairs={{4,0},{8,4},{12,8},{16,12},{20,16},{24,20},{28,24},{5,1},{9,5},{13... | collective-permute-start | bytes 55304 | tf_op jit(solution)/shard_map/ppermute | solution.py:183
  508.5 46.4 %copy-start.48 = (f32[24,768]{1,0:T(8,128)S(1)}, f32[24,768]{1,0:T(8,128)}, u32[]{:S(2)}) copy-start(f32[24,768]{1,0:T(8,128)} %get-tuple-element.236) | copy-start | bytes 221188
  (72 other events, 294.5 us)
Sparse Core Ops, SparseCore 0:
  13.2 144.5 all-gather.2
  160.7 69.7 all-gather.4
  310.2 163.6 reduce-scatter.1
